TPU v7x, 32 devices: a whole 2x2x4 slice. The times are simulated.
32 devices in a mesh: node: 8 (over y, x, core), row: 4 (over z).
Axes of the slice: x: 2, y: 2, z: 4, core: 2. Of those that a mesh axis runs over, the one named last changes fastest.
Arguments:
- samples: bfloat16 [8, 4096, 384], P('node', 'row'), parts along dimension 0, may hold values from -6 to 6
- column_order: int32 [8, 384], P('node'), parts along dimension 0, may hold values from 0 to 383, each once within a row
- skeleton: int32 [8, 256], P('node'), parts along dimension 0, may hold values from 0 to 4095, as said below
Outputs:
- q_factor: float32 [8, 4096, 384], P('node', 'row'), parts along dimension 0
- interp: bfloat16 [8, 4096, 256], P('node', 'row'), parts along dimension 0
There are 8 independent parts, one for each index of `node`. A program takes and returns all parts, laid end to end along the dimension named above; each array names one. Nothing has to cross between parts.
Inputs may be any that keep to these rules, and one draw needn't show every extreme that they name: `skeleton`: each row names 256 distinct sample rows in ascending order. `column_order`: each row is a permutation.
All inputs are finite; a program needn't handle non-finite values.
Results may differ from a plain program's by a relative error of at most 0.001.
Values sent between devices are 32-bit elements; how exact they have to be, the bound alone decides.
No kernel may reach another device: no remote copies, remote signals or barrier semaphores. Data moves between devices by JAX's collectives and lax.ppermute only.
A program may use at most 64 MiB of HBM per device.

v0:
```python
import jax
import jax.numpy as jnp
from jax import lax
from jax.sharding import PartitionSpec as P


def lower_solve(lower, right):
    return jax.scipy.linalg.solve_triangular(lower, right, lower=True)


def upper_solve(lower, right):
    return jax.scipy.linalg.solve_triangular(lower, right, lower=True, trans="T")


def on_device(samples, column_order, skeleton):
    rows_here = samples.shape[1]
    total_rows = rows_here * lax.axis_size("row")
    permuted = jax.vmap(lambda block, order: block[:, order])(samples, column_order)
    gram_local = jnp.einsum("frc,frd->fcd", permuted, permuted, preferred_element_type=jnp.float32)
    offset = lax.axis_index("row") * rows_here
    positions = offset + lax.iota(jnp.int32, rows_here)
    selector = skeleton[:, :, None] == positions[None, None, :]
    picked = jnp.einsum(
        "fkr,frc->fkc", selector.astype(jnp.bfloat16), permuted, preferred_element_type=jnp.float32
    )
    gram, yskel = lax.psum((gram_local, picked), "row")
    lower = jnp.linalg.cholesky(gram / total_rows)
    wide = permuted.astype(jnp.float32)
    q_factor = jnp.swapaxes(jax.vmap(lower_solve)(lower, jnp.swapaxes(wide, 1, 2)), 1, 2)
    qskel = jnp.swapaxes(jax.vmap(lower_solve)(lower, jnp.swapaxes(yskel, 1, 2)), 1, 2)
    small = jnp.einsum("fkc,fjc->fkj", qskel, qskel, precision=lax.Precision.HIGHEST)
    lower_small = jnp.linalg.cholesky(small)
    cross = jnp.einsum("frc,fkc->frk", q_factor, qskel, precision=lax.Precision.HIGHEST)
    inner = jax.vmap(lower_solve)(lower_small, jnp.swapaxes(cross, 1, 2))
    interp = jnp.swapaxes(jax.vmap(upper_solve)(lower_small, inner), 1, 2)
    return (q_factor, interp.astype(jnp.bfloat16))


def solution(mesh):
    placed = (P("node", "row", None), P("node", None), P("node", None))
    return jax.shard_map(
        on_device,
        mesh=mesh,
        in_specs=placed,
        out_specs=(P("node", "row", None), P("node", "row", None)),
        check_vma=False,
    )
```

profile of v0, /device:TPU:0, one launch (start us, length us, event | category | flops | bytes accessed | tf_op | source)
XLA Modules:
  0.0 270.1 jit_solution(1334802724881775004)
XLA Ops:
  7.2 0.7 fusion.43
  7.9 1.4 copy.17
  9.4 4.9 %gather_fusion = bf16[384,1024]{1,0:T(8,128)(2,1)S(1)} fusion(bf16[1,1024,384]{1,2,0:T(8,128)(2,1)S(1)} %copy.17, s32[384]{0:T(512)S(1)} %fusion.47), kind=kCustom, calls=%fused_computation | custom fusion | bytes 1575936 | tf_op jit(solution)/shard_map/vmap()/gather | solution.py:18
  14.3 1.4 convolution_bitcast_fusion
  15.7 1.2 convolution_bitcast_fusion.6
  17.2 52.6 %all-reduce.5.cloned.1.call-done = (f32[1,384,384]{1,2,0:T(8,128)}, f32[1,384,256]{1,2,0:T(8,128)}) async-done(((f32[1,384,384]{1,2,0:T(8,128)}, f32[1,384,256]{1,2,0:T(8,128)}), (f32[1,384,384]{1,2,0:T(8,128)}, f32[1,384,256]{1,2,0:T(8,128)})) %all-reduce.5.cloned.1.call-update) | async-done | bytes 983056 | tf_op jit(solution)/shard_map/psum | solution.py:26
  69.7 2.0 broadcast_multiply_fusion
  71.7 1.3 copy.19
  73.1 0.8 copy-done.1
  73.9 11.7 %custom-call.42 = f32[1,128,128]{2,1,0:T(8,128)S(1)} custom-call(f32[1,128,128]{2,1,0:T(8,128)S(1)} %cholesky.264), custom_call_target="Cholesky" | custom-call | tf_op jit(solution)/shard_map/jit(cholesky)/cholesky | solution.py:27
  85.6 9.8 %custom-call.43 = f32[1,1,128,128]{2,3,1,0:T(8,128)S(1)} custom-call(f32[1,1,128,128]{3,2,1,0:T(8,128)S(1)} %get-tuple-element.55), custom_call_target="InvertDiagBlocksLowerTriangular" | custom-call | tf_op jit(solution)/shard_map/jit(cholesky)/cholesky | solution.py:27
  95.5 1.2 constant_dynamic-update-slice_fusion.3
  96.7 1.2 fusion.12
  97.9 11.7 %custom-call.44 = f32[1,128,128]{2,1,0:T(8,128)S(1)} custom-call(f32[1,128,128]{2,1,0:T(8,128)S(1)} %cholesky.268), custom_call_target="Cholesky" | custom-call | tf_op jit(solution)/shard_map/jit(cholesky)/cholesky | solution.py:27
  109.6 10.4 %custom-call.53 = f32[1,1,128,128]{2,3,1,0:T(8,128)S(1)} custom-call(f32[1,1,128,128]{3,2,1,0:T(8,128)S(1)} %get-tuple-element.52), custom_call_target="InvertDiagBlocksLowerTriangular" | custom-call | tf_op jit(solution)/shard_map/jit(cholesky)/cholesky/custom-call.10 | solution.py:27
  120.2 1.1 fusion.19
  121.3 11.7 %custom-call.45 = f32[1,128,128]{2,1,0:T(8,128)S(1)} custom-call(f32[1,128,128]{2,1,0:T(8,128)S(1)} %fusion.19), custom_call_target="Cholesky" | custom-call | tf_op jit(solution)/shard_map/jit(cholesky)/cholesky | solution.py:27
  133.1 0.7 compare_reduce_fusion.2
  136.5 7.8 %while.2 = (s32[]{:T(128)}, f32[1,384,384]{2,1,0:T(8,128)S(1)}, s32[3,2]{0,1:T(2,128)S(1)}, f32[3,1,128,128]{3,2,1,0:T(8,128)}, s32[]{:T(128)}) while((s32[]{:T(128)}, f32[1,384,384]{2,1,0:T(8,128)S(1)}, s32[3,2]{0,1:T(2,128)S(1)}, f32[3,1,128,128]{3,2,1,0:T(8,128)}, s32[]{:T(128)}) %tuple.49), condition=%wide.while_cond, body=%wide.while_body.sunk | while | flops 2 | bytes 132205 | solution.py:8
  137.1 2.0 bitcast_dynamic-update-slice_fusion.5
  139.7 2.0 bitcast_dynamic-update-slice_fusion.5
  142.3 2.0 bitcast_dynamic-update-slice_fusion.5
  144.3 30.5 %custom-call.46 = f32[1,3,128,128]{2,3,1,0:T(8,128)S(1)} custom-call(f32[1,3,128,128]{3,2,1,0:T(8,128)} %bitcast.260), custom_call_target="InvertDiagBlocksLowerTriangular" | custom-call | tf_op jit(solution)/shard_map/vmap(jit(_solve_triangular))/triangular_solve | solution.py:8
  174.8 1.3 fusion.34
  176.1 1.3 fusion.14
  177.7 1.5 fusion.16
  180.2 0.8 fusion.29
  181.1 0.8 copy.24
  181.9 1.0 fusion.33
  182.9 0.7 copy-done.4
  183.6 11.7 %custom-call.47 = f32[1,128,128]{2,1,0:T(8,128)S(1)} custom-call(f32[1,128,128]{2,1,0:T(8,128)S(1)} %cholesky.272), custom_call_target="Cholesky" | custom-call | tf_op jit(solution)/shard_map/jit(cholesky)/cholesky | solution.py:32
  196.0 1.3 fusion.30
  197.8 1.5 convolution_bitcast_fusion.4
  199.3 0.7 fusion.10
  200.0 1.5 convolution_bitcast_fusion.2
  201.5 2.7 %fusion.2 = f32[1,256,1024]{1,2,0:T(8,128)S(1)} fusion(f32[1,128,1024]{2,1,0:T(8,128)S(1)} %convolution_bitcast_fusion.2, f32[1,128,1024]{2,1,0:T(8,128)S(1)} %convolution_bitcast_fusion.4, f32[1,128,1024]{2,1,0:T(8,128)S(1)} %bitcast.253, f32[1,128,256]{2,1,0:T(8,128)S(1)} %copy-done.3, f32[1,128,256]{2,1,0:T(8,128)S(1)} %convolution_bitcast_fusion.9, ...), kind=kOutput, calls=%fused_computation.8 | convolution fusion | flops 1208942592 | bytes 3014656 | tf_op jit(solution)/shard_map/frc,fkc->frk/dot_general | solution.py:33
  205.1 10.8 %custom-call.54 = f32[1,1,128,128]{2,3,1,0:T(8,128)S(1)} custom-call(f32[1,1,128,128]{3,2,1,0:T(8,128)} %get-tuple-element.48), custom_call_target="InvertDiagBlocksLowerTriangular" | custom-call | tf_op jit(solution)/shard_map/jit(cholesky)/cholesky/custom-call.10 | solution.py:32
  216.4 11.7 %custom-call.48 = f32[1,128,128]{2,1,0:T(8,128)S(1)} custom-call(f32[1,128,128]{2,1,0:T(8,128)S(1)} %fusion.18), custom_call_target="Cholesky" | custom-call | tf_op jit(solution)/shard_map/jit(cholesky)/cholesky | solution.py:32
  228.2 0.6 compare_reduce_fusion
  230.2 5.2 %while.3 = (s32[]{:T(128)}, f32[1,256,256]{2,1,0:T(8,128)S(1)}, s32[2,2]{1,0:T(2,128)S(1)}, f32[2,1,128,128]{3,2,1,0:T(8,128)}, s32[]{:T(128)}) while((s32[]{:T(128)}, f32[1,256,256]{2,1,0:T(8,128)S(1)}, s32[2,2]{1,0:T(2,128)S(1)}, f32[2,1,128,128]{3,2,1,0:T(8,128)}, s32[]{:T(128)}) %tuple.52), condition=%wide.while_cond.1, body=%wide.while_body.1.sunk | while | flops 2 | bytes 132205 | solution.py:12
  230.8 2.0 bitcast_dynamic-update-slice_fusion.6
  233.4 2.0 bitcast_dynamic-update-slice_fusion.6
  235.4 20.7 %custom-call.49 = f32[1,2,128,128]{2,3,1,0:T(8,128)S(1)} custom-call(f32[1,2,128,128]{3,2,1,0:T(8,128)} %bitcast.261), custom_call_target="InvertDiagBlocksLowerTriangular" | custom-call | tf_op jit(solution)/shard_map/vmap(jit(_solve_triangular))/triangular_solve | solution.py:12
  256.8 1.0 fusion.8
  257.8 0.6 fusion.42
  259.1 0.6 convolution_subtract_fusion
  259.8 1.6 copy.27
  262.0 1.0 copy.28
  (63 shorter events, 10.2 us)
Async XLA Ops:
  7.2 62.5 %all-reduce.5.cloned.1.call-start = ((), (), s32[]{:S(2)}) async-start(), calls=%async_computation | async-start | bytes 1966080 | tf_op jit(solution)/shard_map/psum | solution.py:26
  14.3 1.4 copy-start.7
  69.7 3.3 %copy-start = (f32[1,384,384]{1,2,0:T(8,128)S(1)}, f32[1,384,384]{1,2,0:T(8,128)}, u32[]{:S(2)}) copy-start(f32[1,384,384]{1,2,0:T(8,128)} %get-tuple-element.39) | copy-start | bytes 1769476
  73.1 0.8 copy-start.1
  174.8 4.4 %copy-start.6 = (f32[1,3,128,128]{2,3,1,0:T(8,128)}, f32[1,3,128,128]{2,3,1,0:T(8,128)S(1)}, u32[]{:S(2)}) copy-start(f32[1,3,128,128]{2,3,1,0:T(8,128)S(1)} %custom-call.46) | copy-start | bytes 589828
  179.6 0.6 copy-start.2
  182.9 0.7 copy-start.4
  199.3 2.2 copy-start.3
  204.3 11.7 %copy-start.5 = (f32[1,256,256]{2,1,0:T(8,128)S(1)}, f32[1,256,256]{2,1,0:T(8,128)}, u32[]{:S(2)}) copy-start(f32[1,256,256]{2,1,0:T(8,128)} %copy-done.4) | copy-start | bytes 786436
Sparse Core Ops, SparseCore 0:
  17.1 52.5 all-reduce.4
where the time goes:
time: 273 us; the launch traced here: 270 us
  other arithmetic  148 us (54%)
  waiting for transfers between devices  52.6 us (19%)
  local copies, waits for them, and re-layouts  26.4 us (10%)
  matrix products  24.6 us (9%)
  between operations  18 us (7%)
    another operation x10, other arithmetic, on_device(): lower = jnp.linalg.cholesky(gram / total_rows)  56.8 us
    psum x1, waiting for transfers between devices, on_device(): gram, yskel = lax.psum((gram_local, picked), 'row')  52.6 us
    another operation x7, other arithmetic, on_device(): lower_small = jnp.linalg.cholesky(small)  36.2 us
    another operation x3, other arithmetic, lower_solve(): return jax.scipy.linalg.solve_triangular(lower, right, lower=True)  30.5 us
    another operation x4, other arithmetic, upper_solve(): jax.scipy.linalg.solve_triangular(lower, right, lower=True, trans='T')  20.8 us
    another operation x15, local copies, waits for them, and re-layouts  13 us
    another operation x13, matrix products, lower_solve(): return jax.scipy.linalg.solve_triangular(lower, right, lower=True)  12.5 us
    unnamed x19, local copies, waits for them, and re-layouts  6.19 us
  transfers between devices with their start and end apart: 1, of which 1 were waited for; matrix products, arithmetic and copies ran while one was open for 0% of the time, Pallas kernels for 0%

commit v1 on v0

v1 whole, which is shorter than its diff:
```python
import jax
import jax.numpy as jnp
from jax import lax
from jax.experimental import pallas as pl
from jax.experimental.pallas import tpu as pltpu
from jax.sharding import PartitionSpec as P

F32 = jnp.float32
BF16 = jnp.bfloat16
LANES = 128
STRIP = 32
GROUPS = STRIP // 8


def split(x):
    high = x.astype(BF16)
    low = (x - high.astype(F32)).astype(BF16)
    return high, low


def dot(a, b, dims):
    return lax.dot_general(a, b, (dims, ((), ())), preferred_element_type=F32)


NN = ((1,), (0,))
NT = ((1,), (1,))
TN = ((0,), (0,))


def exact_left(a, b, dims):
    high, low = split(b)
    return dot(a, high, dims) + dot(a, low, dims)


def product(a, b, dims):
    ah, al = split(a)
    bh, bl = split(b)
    return dot(ah, bh, dims) + (dot(ah, bl, dims) + dot(al, bh, dims))


def row_of(x, s):
    return jnp.broadcast_to(x[s : s + 1, :], (8, LANES))


def factor_strip(tiles, lane):
    diag = tiles[0]
    cols = [
        [jnp.broadcast_to(diag[g][:, lane + j : lane + j + 1], (8, LANES)) if g >= j // 8 else None for g in range(GROUPS)]
        for j in range(STRIP)
    ]
    tiles = [list(t) for t in tiles]
    sub = lax.broadcasted_iota(jnp.int32, (8, LANES), 0)
    for k in range(STRIP):
        g0, s = divmod(k, 8)
        inv = lax.rsqrt(row_of(cols[k][g0], s))
        low = [cols[k][g] * inv if g >= g0 else None for g in range(GROUPS)]
        for j in range(k + 1, STRIP):
            factor = row_of(low[j // 8], j % 8)
            for g in range(j // 8, GROUPS):
                cols[j][g] = cols[j][g] - low[g] * factor
        below = jnp.where(sub > s, low[g0], 0.0)
        for t in tiles:
            row = row_of(t[g0], s) * inv
            t[g0] = jnp.where(sub == s, row, t[g0] - below * row)
            for g in range(g0 + 1, GROUPS):
                t[g] = t[g] - low[g] * row
    return tiles


def factor(a_ref, t_ref, n):
    tiles_n = n // LANES
    row_ids = lax.broadcasted_iota(jnp.int32, (LANES, LANES), 0)
    col_ids = lax.broadcasted_iota(jnp.int32, (LANES, LANES), 1)
    for i in range(tiles_n):
        for j in range(tiles_n):
            t_ref[LANES * i : LANES * (i + 1), LANES * j : LANES * (j + 1)] = (
                jnp.where(row_ids == col_ids, 1.0, 0.0) if i == j else jnp.zeros((LANES, LANES), F32)
            )

    def spots(panel):
        return [(a_ref, t) for t in range(panel, tiles_n)] + [(t_ref, t) for t in range(panel + 1)]

    def update(rows, panel, first, last):
        size = rows.stop - rows.start
        left = a_ref[first:last, rows]
        lh, ll = split(left)
        left3 = jnp.concatenate([lh, lh, ll], axis=0)
        where = spots(panel)
        right = [split(ref[first:last, LANES * t : LANES * (t + 1)]) for ref, t in where]
        right3 = jnp.concatenate(
            [jnp.concatenate([h, l, h], axis=0) for h, l in right], axis=1
        )
        out = dot(left3, right3, TN)
        for i, (ref, t) in enumerate(where):
            at = slice(LANES * t, LANES * (t + 1))
            ref[rows, at] = ref[rows, at] - out[:, LANES * i : LANES * (i + 1)]

    per = LANES // STRIP
    for panel in range(tiles_n):
        base = LANES * panel
        for strip in range(per):
            r0 = base + STRIP * strip
            where = spots(panel)
            tiles = [
                [ref[r0 + 8 * g : r0 + 8 * g + 8, LANES * t : LANES * (t + 1)] for g in range(GROUPS)] for ref, t in where
            ]
            tiles = factor_strip(tiles, STRIP * strip)
            for (ref, t), tile in zip(where, tiles):
                for g in range(GROUPS):
                    ref[r0 + 8 * g : r0 + 8 * g + 8, LANES * t : LANES * (t + 1)] = tile[g]
            if strip + 1 < per:
                update(slice(r0 + STRIP, base + LANES), panel, r0, r0 + STRIP)
        if panel + 1 < tiles_n:
            update(slice(base + LANES, n), panel, base, base + LANES)


def upper_blocks(count):
    return [(i, j) for i in range(count) for j in range(i, count)]


def block(i):
    return slice(LANES * i, LANES * (i + 1))


def gram_kernel(order_ref, x_ref, p_ref, g_ref):
    c = x_ref.shape[1]
    source = lax.broadcasted_iota(jnp.int32, (c, c), 0)
    select = jnp.where(source == order_ref[0:1, :], 1.0, 0.0).astype(BF16)
    p = dot(x_ref[...], select, NN).astype(BF16)
    p_ref[...] = p
    for at, (i, j) in enumerate(upper_blocks(c // LANES)):
        g_ref[at] = dot(p[:, block(i)], p[:, block(j)], TN)


def pick_kernel(offset_ref, skel_ref, p_ref, y_ref):
    rows = p_ref.shape[0]
    k = skel_ref.shape[0]
    here = lax.broadcasted_iota(jnp.int32, (k, rows), 1) + offset_ref[0]
    select = jnp.where(here == skel_ref[:, 0:1], 1.0, 0.0).astype(BF16)
    y_ref[...] = dot(select, p_ref[...], NN)


def make_factor_kernel(total_rows):
    def factor_kernel(g_ref, h_ref, t_ref, a_ref):
        c = t_ref.shape[0]
        for at, (i, j) in enumerate(upper_blocks(c // LANES)):
            a_ref[block(i), block(j)] = (g_ref[at] + h_ref[at]) * (1.0 / total_rows)
        factor(a_ref, t_ref, c)

    return factor_kernel


def finish_kernel(p_ref, t_ref, y_ref, z_ref, q_ref, w_ref, a_ref, s_ref):
    k = y_ref.shape[0]
    t = t_ref[...]
    y = (y_ref[...] + z_ref[...]).astype(BF16)
    p = p_ref[...]
    qskel = exact_left(y, t, NT)
    a_ref[...] = product(qskel, qskel, NT)
    q = exact_left(p, t, NT)
    q_ref[...] = q
    cross = product(q, qskel, NT)
    factor(a_ref, s_ref, k)
    s = s_ref[...]
    inverse = product(s, s, TN)
    w_ref[...] = product(cross, inverse, NN).astype(BF16)


def vmem(shape, dtype):
    return pltpu.VMEM(shape, dtype)


PARAMS = pltpu.CompilerParams(vmem_limit_bytes=48 * 1024 * 1024)


def rounds(size):
    out, width = [], 2
    while width <= size:
        out.append([(i, i - i % width + width - 1 - i % width) for i in range(size)])
        width *= 2
    return out


def swap(x, pairs):
    return lax.ppermute(x, "row", pairs)


def on_device(samples, column_order, skeleton):
    fronts, rows, c = samples.shape
    k = skeleton.shape[1]
    size = lax.axis_size("row")
    total_rows = rows * size
    offset = (lax.axis_index("row") * rows).astype(jnp.int32).reshape(1)
    q_all, w_all = [], []
    for f in range(fronts):
        count = len(upper_blocks(c // LANES))
        p, gram = pl.pallas_call(
            gram_kernel,
            out_shape=(jax.ShapeDtypeStruct((rows, c), BF16), jax.ShapeDtypeStruct((count, LANES, LANES), F32)),
            compiler_params=PARAMS,
            name="gram",
        )(jnp.broadcast_to(column_order[f][None, :], (8, c)), samples[f])
        y = pl.pallas_call(
            pick_kernel,
            in_specs=[pl.BlockSpec(memory_space=pltpu.SMEM), pl.BlockSpec(), pl.BlockSpec()],
            out_shape=jax.ShapeDtypeStruct((k, c), F32),
            compiler_params=PARAMS,
            name="pick",
        )(offset, jnp.broadcast_to(skeleton[f][:, None], (k, LANES)), p)
        steps = rounds(size)
        for at, pairs in enumerate(steps):
            gram_in = swap(gram, pairs)
            if at + 1 < len(steps):
                gram = gram + gram_in
        for at, pairs in enumerate(steps):
            y_in = swap(y, pairs)
            if at + 1 < len(steps):
                y = y + y_in
        t = pl.pallas_call(
            make_factor_kernel(total_rows),
            out_shape=jax.ShapeDtypeStruct((c, c), F32),
            scratch_shapes=[vmem((c, c), F32)],
            compiler_params=PARAMS,
            name="factor",
        )(gram, gram_in)
        q, w = pl.pallas_call(
            finish_kernel,
            out_shape=(jax.ShapeDtypeStruct((rows, c), F32), jax.ShapeDtypeStruct((rows, k), BF16)),
            scratch_shapes=[vmem((k, k), F32), vmem((k, k), F32)],
            compiler_params=PARAMS,
            name="finish",
        )(p, t, y, y_in)
        q_all.append(q)
        w_all.append(w)
    return jnp.stack(q_all), jnp.stack(w_all)


def solution(mesh):
    placed = (P("node", "row", None), P("node", None), P("node", None))
    return jax.shard_map(
        on_device,
        mesh=mesh,
        in_specs=placed,
        out_specs=(P("node", "row", None), P("node", "row", None)),
        check_vma=False,
    )
```

time: 273 us -> 61.7 us (0.23)
  other arithmetic: 148 us -> 0.78 us
  waiting for transfers between devices: 52.6 us -> 12.4 us
  matrix products: 24.6 us -> 0 us
  local copies, waits for them, and re-layouts: 26.4 us -> 1.9 us
  starting transfers between devices: 0.04 us -> 23.4 us
  Pallas kernels: 0 us -> 22.4 us
  between operations: 18 us -> 0.68 us
    another operation x24 -> x0, other arithmetic: 144 us -> none  [the longest x10 56.8 us: on_device(): lower = jnp.linalg.cholesky(gram / total_rows)]
    psum x1 -> x0, waiting for transfers between devices: 52.6 us -> none  [on_device(): gram, yskel = lax.psum((gram_local, picked), 'row')]
    ppermute x0 -> x4, starting transfers between devices: none -> 23.4 us  [swap(): return lax.ppermute(x, 'row', pairs)]
    pallas_call x0 -> x4, Pallas kernels: none -> 22.4 us  [the longest x1 10.5 us: on_device(): pl.pallas_call(make_factor_kernel(total_rows), out_shape=jax.ShapeDtypeSt...]
    another operation x22 -> x0, matrix products: 18.4 us -> none  [the longest x13 12.5 us: lower_solve(): return jax.scipy.linalg.solve_triangular(lower, right, lower=True)]
    another operation x22 -> x0, local copies, waits for them, and re-layouts: 13.2 us -> none
    ppermute x0 -> x4, waiting for transfers between devices: none -> 12.4 us  [swap(): return lax.ppermute(x, 'row', pairs)]
    dot_general x4 -> x0, matrix products: 6.22 us -> none  [the longest x1 2.73 us: on_device(): jnp.einsum('frc,fkc->frk', q_factor, qskel, precision=lax.Precision.HIGHEST)]
  transfers between devices with their start and end apart: 1 -> 4, of which waited for: 1 -> 2; matrix products, arithmetic and copies ran while one was open for 0% -> 1% of each run, Pallas kernels for 0% -> 18%
where the time goes in v1:
time: 61.7 us; the launch traced here: 61.5 us
  starting transfers between devices  23.4 us (38%)
  Pallas kernels  22.4 us (36%)
  waiting for transfers between devices  12.4 us (20%)
  local copies, waits for them, and re-layouts  1.9 us (3%)
  other arithmetic  0.78 us (1%)
  between operations  0.68 us (1%)
    ppermute x4, starting transfers between devices, swap(): return lax.ppermute(x, 'row', pairs)  23.4 us
    ppermute x4, waiting for transfers between devices, swap(): return lax.ppermute(x, 'row', pairs)  12.4 us
    pallas_call x1, Pallas kernels, on_device(): pl.pallas_call(make_factor_kernel(total_rows), out_shape=jax.ShapeDtypeSt...  10.5 us
    pallas_call x1, Pallas kernels, on_device(): pl.pallas_call(finish_kernel, out_shape=(jax.ShapeDtypeStruct((rows, c),...  10.1 us
    pallas_call x1, Pallas kernels, on_device(): pl.pallas_call(gram_kernel, out_shape=(jax.ShapeDtypeStruct((rows, c), BF...  1.27 us
  transfers between devices with their start and end apart: 4, of which 2 were waited for; matrix products, arithmetic and copies ran while one was open for 1% of the time, Pallas kernels for 18%

profile of v1, /device:TPU:0, one launch (start us, length us, event | category | flops | bytes accessed | tf_op | source)
XLA Modules:
  0.0 61.5 jit_solution(4300651215035238809)
XLA Ops:
  0.6 0.7 %reduce = s32[384]{0:T(512)S(1)} reduce(s32[1,384]{1,0:T(1,128)} %param.4, s32[]{:T(128)} %constant.9), dimensions={0}, to_apply=%param.4.reduce_sub_computation | reduce | bytes 3076 | tf_op args[1]
  1.3 0.0 copy-start
  1.3 1.1 %copy-done = bf16[1,1024,384]{2,1,0:T(8,128)(2,1)S(1)} copy-done((bf16[1,1024,384]{2,1,0:T(8,128)(2,1)S(1)}, bf16[1,1024,384]{2,1,0:T(8,128)(2,1)}, u32[]{:S(2)}) %copy-start) | copy-done | bytes 786456
  2.5 1.3 %gram.1 = (bf16[1024,384]{1,0:T(8,128)(2,1)S(1)}, f32[6,128,128]{2,1,0:T(8,128)S(1)}) custom-call(s32[8,384]{1,0:T(8,128)S(1)} %broadcast_in_dim.15.order_ref, bf16[1024,384]{1,0:T(8,128)(2,1)S(1)} %bitcast.5), custom_call_target="tpu_custom_call" | custom-call | tf_op jit(solution)/shard_map/gram/pallas_call | solution.py:197
  3.7 3.1 %collective-permute-start = (f32[6,128,128]{2,1,0:T(8,128)S(1)}, f32[6,128,128]{2,1,0:T(8,128)S(1)}, u32[]{:S(2)}, u32[]{:S(2)}) collective-permute-start(f32[6,128,128]{2,1,0:T(8,128)S(1)} %get-tuple-element.7), channel_id=1, source_target_pairs={{0,1},{1,0},{2,3},{3,2},{4,5},{5,4},{6,7},{7,6},{8,9},{9,8},{10,11... | collective-permute-start | bytes 1179656 | tf_op jit(solution)/shard_map/ppermute | solution.py:185
  6.9 0.8 %broadcast_in_dim.17.skel_ref = s32[256,128]{1,0:T(8,128)S(1)} broadcast(s32[256]{0:T(256)} %bitcast.6), dimensions={0} | broadcast | bytes 132096 | tf_op jit(solution)/shard_map/broadcast_in_dim | solution.py:209
  7.6 0.5 pick.1
  8.1 0.1 collective-permute-start.2
  8.2 8.6 %collective-permute-done = f32[6,128,128]{2,1,0:T(8,128)S(1)} collective-permute-done((f32[6,128,128]{2,1,0:T(8,128)S(1)}, f32[6,128,128]{2,1,0:T(8,128)S(1)}, u32[]{:S(2)}, u32[]{:S(2)}) %collective-permute-start) | collective-permute-done | bytes 393248 | tf_op jit(solution)/shard_map/ppermute | solution.py:185
  16.9 4.1 %collective-permute-start.1 = (f32[6,128,128]{2,1,0:T(8,128)S(1)}, f32[6,128,128]{2,1,0:T(8,128)S(1)}, u32[]{:S(2)}, u32[]{:S(2)}) collective-permute-start(f32[6,128,128]{2,1,0:T(8,128)S(1)} %add.6.g_ref), channel_id=1, source_target_pairs={{0,3},{1,2},{2,1},{3,0},{4,7},{5,6},{6,5},{7,4},{8,11},{9,10},{10,... | collective-permute-start | bytes 1179656 | tf_op jit(solution)/shard_map/ppermute | solution.py:185
  21.0 3.8 %collective-permute-done.2 = f32[256,384]{1,0:T(8,128)S(1)} collective-permute-done((f32[256,384]{1,0:T(8,128)S(1)}, f32[256,384]{1,0:T(8,128)S(1)}, u32[]{:S(2)}, u32[]{:S(2)}) %collective-permute-start.2) | collective-permute-done | bytes 393248 | tf_op jit(solution)/shard_map/ppermute | solution.py:185
  24.8 16.1 %collective-permute-start.3 = (f32[256,384]{1,0:T(8,128)S(1)}, f32[256,384]{1,0:T(8,128)S(1)}, u32[]{:S(2)}, u32[]{:S(2)}) collective-permute-start(f32[256,384]{1,0:T(8,128)S(1)} %add.7.y_ref), channel_id=1, source_target_pairs={{0,3},{1,2},{2,1},{3,0},{4,7},{5,6},{6,5},{7,4},{8,11},{9,10},{10,... | collective-permute-start | bytes 1179656 | tf_op jit(solution)/shard_map/ppermute | solution.py:185
  40.9 0.0 collective-permute-done.1.h_ref
  40.9 10.5 %factor.1.t_ref = f32[384,384]{1,0:T(8,128)S(1)} custom-call(f32[6,128,128]{2,1,0:T(8,128)S(1)} %add.6.g_ref, f32[6,128,128]{2,1,0:T(8,128)S(1)} %collective-permute-done.1.h_ref), custom_call_target="tpu_custom_call" | custom-call | tf_op jit(solution)/shard_map/factor/pallas_call | solution.py:219
  51.4 0.0 collective-permute-done.3.z_ref
  51.4 10.1 %finish.1 = (f32[1024,384]{1,0:T(8,128)}, bf16[1024,256]{1,0:T(8,128)(2,1)}) custom-call(bf16[1024,384]{1,0:T(8,128)(2,1)S(1)} %get-tuple-element.6.p_ref, f32[384,384]{1,0:T(8,128)S(1)} %factor.1.t_ref, f32[256,384]{1,0:T(8,128)S(1)} %add.7.y_ref, f32[256,384]{1,0:T(8,128)S(1)} %collective-permute-done.3.z_ref), custom_call_target="tpu_custom_call" | custom-call | tf_op jit(solution)/shard_map/finish/pallas_call | solution.py:226
  (3 shorter events, 0.1 us)
Async XLA Ops:
  1.3 1.1 %copy-start = (bf16[1,1024,384]{2,1,0:T(8,128)(2,1)S(1)}, bf16[1,1024,384]{2,1,0:T(8,128)(2,1)}, u32[]{:S(2)}) copy-start(bf16[1,1024,384]{2,1,0:T(8,128)(2,1)} %param.3) | copy-start | bytes 2359300
  3.7 13.1 %collective-permute-start = (f32[6,128,128]{2,1,0:T(8,128)S(1)}, f32[6,128,128]{2,1,0:T(8,128)S(1)}, u32[]{:S(2)}, u32[]{:S(2)}) collective-permute-start(f32[6,128,128]{2,1,0:T(8,128)S(1)} %get-tuple-element.7), channel_id=1, source_target_pairs={{0,1},{1,0},{2,3},{3,2},{4,5},{5,4},{6,7},{7,6},{8,9},{9,8},{10,11... | collective-permute-start | bytes 1179656 | tf_op jit(solution)/shard_map/ppermute | solution.py:185
  8.1 16.7 %collective-permute-start.2 = (f32[256,384]{1,0:T(8,128)S(1)}, f32[256,384]{1,0:T(8,128)S(1)}, u32[]{:S(2)}, u32[]{:S(2)}) collective-permute-start(f32[256,384]{1,0:T(8,128)S(1)} %pick.1), channel_id=1, source_target_pairs={{0,1},{1,0},{2,3},{3,2},{4,5},{5,4},{6,7},{7,6},{8,9},{9,8},{10,11... | collective-permute-start | bytes 1179656 | tf_op jit(solution)/shard_map/ppermute | solution.py:185
  16.9 24.0 %collective-permute-start.1 = (f32[6,128,128]{2,1,0:T(8,128)S(1)}, f32[6,128,128]{2,1,0:T(8,128)S(1)}, u32[]{:S(2)}, u32[]{:S(2)}) collective-permute-start(f32[6,128,128]{2,1,0:T(8,128)S(1)} %add.6.g_ref), channel_id=1, source_target_pairs={{0,3},{1,2},{2,1},{3,0},{4,7},{5,6},{6,5},{7,4},{8,11},{9,10},{10,... | collective-permute-start | bytes 1179656 | tf_op jit(solution)/shard_map/ppermute | solution.py:185
  24.8 26.6 %collective-permute-start.3 = (f32[256,384]{1,0:T(8,128)S(1)}, f32[256,384]{1,0:T(8,128)S(1)}, u32[]{:S(2)}, u32[]{:S(2)}) collective-permute-start(f32[256,384]{1,0:T(8,128)S(1)} %add.7.y_ref), channel_id=1, source_target_pairs={{0,3},{1,2},{2,1},{3,0},{4,7},{5,6},{6,5},{7,4},{8,11},{9,10},{10,... | collective-permute-start | bytes 1179656 | tf_op jit(solution)/shard_map/ppermute | solution.py:185

commit v2 on v0

v2 whole, which is shorter than its diff:
```python
import jax
import jax.numpy as jnp
from jax import lax
from jax.experimental import pallas as pl
from jax.experimental.pallas import tpu as pltpu
from jax.sharding import PartitionSpec as P


F32 = jnp.float32
BF16 = jnp.bfloat16
LANES = 128
STRIP = 32
GROUPS = STRIP // 8


def split(x):
    high = x.astype(BF16)
    low = (x - high.astype(F32)).astype(BF16)
    return high, low


def dot(a, b, dims):
    return lax.dot_general(a, b, (dims, ((), ())), preferred_element_type=F32)


NN = ((1,), (0,))
NT = ((1,), (1,))
TN = ((0,), (0,))


def exact_left(a, b, dims):
    high, low = split(b)
    return dot(a, high, dims) + dot(a, low, dims)


def product(a, b, dims):
    ah, al = split(a)
    bh, bl = split(b)
    return dot(ah, bh, dims) + (dot(ah, bl, dims) + dot(al, bh, dims))


def row_of(x, s):
    return jnp.broadcast_to(x[s : s + 1, :], (8, LANES))


def factor_strip(tiles, lane):
    diag = tiles[0]
    cols = [
        [jnp.broadcast_to(diag[g][:, lane + j : lane + j + 1], (8, LANES)) if g >= j // 8 else None for g in range(GROUPS)]
        for j in range(STRIP)
    ]
    tiles = [list(t) for t in tiles]
    sub = lax.broadcasted_iota(jnp.int32, (8, LANES), 0)
    for k in range(STRIP):
        g0, s = divmod(k, 8)
        inv = lax.rsqrt(row_of(cols[k][g0], s))
        low = [cols[k][g] * inv if g >= g0 else None for g in range(GROUPS)]
        for j in range(k + 1, STRIP):
            factor = row_of(low[j // 8], j % 8)
            for g in range(j // 8, GROUPS):
                cols[j][g] = cols[j][g] - low[g] * factor
        below = jnp.where(sub > s, low[g0], 0.0)
        for t in tiles:
            row = row_of(t[g0], s) * inv
            t[g0] = jnp.where(sub == s, row, t[g0] - below * row)
            for g in range(g0 + 1, GROUPS):
                t[g] = t[g] - low[g] * row
    return tiles


def block(i):
    return slice(LANES * i, LANES * (i + 1))


def set_identity(ref):
    row_ids = lax.broadcasted_iota(jnp.int32, (LANES, LANES), 0)
    col_ids = lax.broadcasted_iota(jnp.int32, (LANES, LANES), 1)
    last = ref.shape[1] // LANES - 1
    for j in range(last):
        ref[:, block(j)] = jnp.zeros((LANES, LANES), F32)
    ref[:, block(last)] = jnp.where(row_ids == col_ids, 1.0, 0.0)


def stack_left(x):
    high, low = split(x)
    return [high, high, low]


def stack_right(x):
    high, low = split(x)
    return [high, low, high]


def take_out(ref, rows, t, lefts, rights):
    left = jnp.concatenate([part for x in lefts for part in x], axis=0)
    right = jnp.concatenate([part for x in rights for part in stack_right(x)], axis=0)
    ref[rows, block(t)] = ref[rows, block(t)] - dot(left, right, TN)


def factor_panel(u_ref, t_ref):
    targets = [(u_ref, t) for t in range(u_ref.shape[1] // LANES)]
    targets += [(t_ref, t) for t in range(t_ref.shape[1] // LANES)]
    for r0 in range(0, LANES, STRIP):
        tiles = [[ref[r0 + 8 * g : r0 + 8 * g + 8, block(t)] for g in range(GROUPS)] for ref, t in targets]
        tiles = factor_strip(tiles, r0)
        for (ref, t), tile in zip(targets, tiles):
            for g in range(GROUPS):
                ref[r0 + 8 * g : r0 + 8 * g + 8, block(t)] = tile[g]
        if r0 + STRIP < LANES:
            rows = slice(r0 + STRIP, LANES)
            whole = [jnp.concatenate(tile, axis=0) for tile in tiles]
            left = stack_left(whole[0][:, r0 + STRIP :])
            for (ref, t), right in zip(targets, whole):
                take_out(ref, rows, t, [left], [right])


def take_out_panels(u_before, t_before, u_ref, t_ref):
    panel = len(u_before)
    if not panel:
        return
    rows = slice(0, LANES)
    lefts = [stack_left(u_before[at][:, block(panel - at)]) for at in range(panel)]
    for i in range(u_ref.shape[1] // LANES):
        take_out(u_ref, rows, i, lefts, [u_before[at][:, block(panel - at + i)] for at in range(panel)])
    for i in range(panel):
        take_out(t_ref, rows, i, lefts[i:], [t_before[at][:, block(i)] for at in range(i, panel)])


def upper_blocks(first, count):
    return [(i, j) for i in range(first, count) for j in range(i, count)]


PACKED_ROWS = LANES // 2


def pack_list(count):
    return [(i, j) for i, j in upper_blocks(0, count) if i != j or i > 1]


def message_rows(count):
    return PACKED_ROWS * (1 + len(pack_list(count))) + 8


def masks():
    row_ids = lax.broadcasted_iota(jnp.int32, (LANES, LANES), 0)
    col_ids = lax.broadcasted_iota(jnp.int32, (LANES, LANES), 1)
    return row_ids, col_ids


def gram_kernel(place_ref, order_ref, x_ref, p_ref, keep_ref, send_ref):
    c = x_ref.shape[1]
    count = c // LANES
    source = lax.broadcasted_iota(jnp.int32, (c, c), 0)
    select = jnp.where(source == order_ref[0:1, :], 1.0, 0.0).astype(BF16)
    p = dot(x_ref[...], select, NN).astype(BF16)
    p_ref[...] = p
    even = place_ref[1] == 0
    row_ids, col_ids = masks()

    def put(at, g):
        top, low = g[:PACKED_ROWS], g[PACKED_ROWS:]
        keep_ref[PACKED_ROWS * at : PACKED_ROWS * (at + 1)] = jnp.where(even, top, low)
        send_ref[PACKED_ROWS * at : PACKED_ROWS * (at + 1)] = jnp.where(even, low, top)

    d0 = dot(p[:, block(0)], p[:, block(0)], TN)
    d1 = dot(p[:, block(1)], p[:, block(1)], TN)
    put(0, jnp.where(row_ids >= col_ids, d0, d1))
    diagonal = jnp.sum(jnp.where(row_ids == col_ids, d1, 0.0), axis=0, keepdims=True)
    diagonal = jnp.broadcast_to(diagonal, (8, LANES))
    for ref in (keep_ref, send_ref):
        ref[ref.shape[0] - 8 :] = diagonal
    for at, (i, j) in enumerate(pack_list(count)):
        put(at + 1, dot(p[:, block(i)], p[:, block(j)], TN))


def unpack(even, mine_ref, other_ref, count, scale):
    def take(at):
        return join(
            even,
            mine_ref[PACKED_ROWS * at : PACKED_ROWS * (at + 1)],
            other_ref[PACKED_ROWS * at : PACKED_ROWS * (at + 1)],
        ) * scale

    row_ids, col_ids = masks()
    shared = take(0)
    turned = shared.T
    diagonal = mine_ref[mine_ref.shape[0] - 8 :][0:1] * scale
    out = {
        (0, 0): jnp.where(row_ids >= col_ids, shared, turned),
        (1, 1): jnp.where(row_ids < col_ids, shared, jnp.where(row_ids > col_ids, turned, diagonal)),
    }
    for at, spot in enumerate(pack_list(count)):
        out[spot] = take(at + 1)
    return out


def pick_kernel(place_ref, skel_ref, p_ref, keep_ref, send_ref):
    rows = p_ref.shape[0]
    k = skel_ref.shape[1]
    here = lax.broadcasted_iota(jnp.int32, (rows, k), 0) + place_ref[0]
    select = jnp.where(here == skel_ref[0:1, :], 1.0, 0.0).astype(BF16)
    y = dot(select, p_ref[...], TN)
    even = place_ref[1] == 0
    keep_ref[...] = jnp.where(even, y[: k // 2], y[k // 2 :])
    send_ref[...] = jnp.where(even, y[k // 2 :], y[: k // 2])


def join(even, mine, other):
    return jnp.concatenate([jnp.where(even, mine, other), jnp.where(even, other, mine)], axis=-2)


def make_panels_kernel(first, last, count, total_rows):
    def panels_kernel(place_ref, mine_ref, other_ref, *refs):
        us, ts = list(refs[:first]), list(refs[first : 2 * first])
        us += refs[2 * first : first + last]
        ts += refs[first + last :]
        gram = unpack(place_ref[1] == 0, mine_ref, other_ref, count, 1.0 / total_rows)
        for panel in range(first, last):
            for j in range(panel, count):
                us[panel][:, block(j - panel)] = gram[panel, j]
            set_identity(ts[panel])
            take_out_panels(us[:panel], ts[:panel], us[panel], ts[panel])
            factor_panel(us[panel], ts[panel])

    return panels_kernel


def finish_kernel(place_ref, p_ref, mine_ref, other_ref, *refs):
    t_parts = refs[:-5]
    q_ref, w_ref, tt_ref, a_ref, s_ref = refs[-5:]
    even = place_ref[1] == 0
    k = a_ref.shape[0]
    for i, part in enumerate(t_parts):
        tt_ref[block(i), : part.shape[1]] = part[...]
        if i + 1 < len(t_parts):
            tt_ref[block(i), part.shape[1] :] = jnp.zeros((LANES, tt_ref.shape[1] - part.shape[1]), F32)
    t = tt_ref[...]
    y = join(even, mine_ref[...], other_ref[...]).astype(BF16)
    p = p_ref[...]
    qskel = exact_left(y, t, NT)
    a_ref[...] = product(qskel, qskel, NT)
    q = exact_left(p, t, NT)
    q_ref[...] = q
    cross = product(q, qskel, NT)
    panels = k // LANES
    us = [a_ref.at[block(i), LANES * i :] for i in range(panels)]
    ts = [s_ref.at[block(i), : LANES * (i + 1)] for i in range(panels)]
    for i in range(panels):
        set_identity(ts[i])
        if i + 1 < panels:
            s_ref[block(i), LANES * (i + 1) :] = jnp.zeros((LANES, k - LANES * (i + 1)), F32)
        take_out_panels(us[:i], ts[:i], us[i], ts[i])
        factor_panel(us[i], ts[i])
    s = s_ref[...]
    inverse = product(s, s, TN)
    w_ref[...] = product(cross, inverse, NN).astype(BF16)


def vmem(shape, dtype):
    return pltpu.VMEM(shape, dtype)


PARAMS = pltpu.CompilerParams(vmem_limit_bytes=48 * 1024 * 1024)


def call(kernel, out_shape, place, *args, scratch=()):
    return pl.pallas_call(
        kernel,
        in_specs=[pl.BlockSpec(memory_space=pltpu.SMEM)] + [pl.BlockSpec()] * len(args),
        out_shape=out_shape,
        scratch_shapes=scratch,
        compiler_params=PARAMS,
    )(place, *args)


def shape(*dims, dtype=F32):
    return jax.ShapeDtypeStruct(dims, dtype)


def swap(x, pairs):
    return lax.ppermute(x, "row", pairs)


def neighbours(size):
    return [(i, i ^ 1) for i in range(size)]


def mirrored(size, width):
    return [(i, i ^ (width - 1)) for i in range(size)]


def share(keep, send, size):
    got = swap(send, neighbours(size))
    mine = keep + got
    width = 4
    while width <= size:
        got = swap(mine, mirrored(size, width))
        mine = mine + got
        width *= 2
    other = swap(mine, neighbours(size))
    return mine, other


def compute(samples, column_order, skeleton):
    fronts, rows, c = samples.shape
    k = skeleton.shape[1]
    size = lax.axis_size("row")
    total_rows = rows * size
    index = lax.axis_index("row")
    place = jnp.stack([index * rows, (index ^ (index >> 1)) & 1]).astype(jnp.int32)
    count = c // LANES
    q_all, w_all = [], []
    for f in range(fronts):
        p, keep, sent = call(
            gram_kernel,
            (shape(rows, c, dtype=BF16),) + (shape(message_rows(count), LANES),) * 2,
            place,
            column_order[f][None, :],
            samples[f],
        )
        keep_y, sent_y = call(pick_kernel, (shape(k // 2, c),) * 2, place, skeleton[f][None, :], p)
        mine, other = share(keep, sent, size)
        mine_y, other_y = share(keep_y, sent_y, size)
        us, ts = [], []
        cut = count - 1
        for first, last in ((0, cut), (cut, count)):
            out = call(
                make_panels_kernel(first, last, count, total_rows),
                tuple(shape(LANES, c - LANES * i) for i in range(first, last))
                + tuple(shape(LANES, LANES * (i + 1)) for i in range(first, last)),
                place,
                mine,
                other,
                *us,
                *ts,
            )
            us += out[: last - first]
            ts += out[last - first :]
        q, w = call(
            finish_kernel,
            (shape(rows, c), shape(rows, k, dtype=BF16)),
            place,
            p,
            mine_y,
            other_y,
            *ts,
            scratch=[vmem((c, c), F32), vmem((k, k), F32), vmem((k, k), F32)],
        )
        q_all.append(q)
        w_all.append(w)
    return jnp.stack(q_all), jnp.stack(w_all)


def solution(mesh):
    placed = (P("node", "row", None), P("node", None), P("node", None))
    return jax.shard_map(
        compute,
        mesh=mesh,
        in_specs=placed,
        out_specs=(P("node", "row", None), P("node", "row", None)),
        check_vma=False,
    )
```

time: 273 us -> 61.2 us (0.22)
  other arithmetic: 148 us -> 0.16 us
  waiting for transfers between devices: 52.6 us -> 12.2 us
  Pallas kernels: 0 us -> 25.5 us
  matrix products: 24.6 us -> 0 us
  local copies, waits for them, and re-layouts: 26.4 us -> 2.49 us
  starting transfers between devices: 0.04 us -> 20 us
  between operations: 18 us -> 0.68 us
    another operation x24 -> x1, other arithmetic: 144 us -> 0.08 us  [compute(): jnp.stack([index * rows, (index ^ index >> 1) & 1]).astype(jnp.int32)]
    psum x1 -> x0, waiting for transfers between devices: 52.6 us -> none  [on_device(): gram, yskel = lax.psum((gram_local, picked), 'row')]
    pallas_call x0 -> x5, Pallas kernels: none -> 25.5 us  [call(): pl.pallas_call(kernel, in_specs=[pl.BlockSpec(memory_space=pltpu.SMEM)] +...]
    ppermute x0 -> x6, starting transfers between devices: none -> 20 us  [swap(): return lax.ppermute(x, 'row', pairs)]
    another operation x22 -> x0, matrix products: 18.4 us -> none  [the longest x13 12.5 us: lower_solve(): return jax.scipy.linalg.solve_triangular(lower, right, lower=True)]
    another operation x22 -> x0, local copies, waits for them, and re-layouts: 13.2 us -> none
    ppermute x0 -> x6, waiting for transfers between devices: none -> 12.2 us  [swap(): return lax.ppermute(x, 'row', pairs)]
    dot_general x4 -> x0, matrix products: 6.22 us -> none  [the longest x1 2.73 us: on_device(): jnp.einsum('frc,fkc->frk', q_factor, qskel, precision=lax.Precision.HIGHEST)]
  transfers between devices with their start and end apart: 1 -> 6, of which waited for: 1 -> 3; matrix products, arithmetic and copies ran while one was open for 0% -> 0% of each run, Pallas kernels for 0% -> 20%
where the time goes in v2:
time: 61.2 us; the launch traced here: 61 us
  Pallas kernels  25.5 us (42%)
  starting transfers between devices  20 us (33%)
  waiting for transfers between devices  12.2 us (20%)
  local copies, waits for them, and re-layouts  2.49 us (4%)
  between operations  0.68 us (1%)
    pallas_call x5, Pallas kernels, call(): pl.pallas_call(kernel, in_specs=[pl.BlockSpec(memory_space=pltpu.SMEM)] +...  25.5 us
    ppermute x6, starting transfers between devices, swap(): return lax.ppermute(x, 'row', pairs)  20 us
    ppermute x6, waiting for transfers between devices, swap(): return lax.ppermute(x, 'row', pairs)  12.2 us
    unnamed x6, local copies, waits for them, and re-layouts  2.49 us
  transfers between devices with their start and end apart: 6, of which 3 were waited for; matrix products, arithmetic and copies ran while one was open for 0% of the time, Pallas kernels for 20%

profile of v2, /device:TPU:0, one launch (start us, length us, event | category | flops | bytes accessed | tf_op | source)
XLA Modules:
  0.0 61.0 jit_solution(18374626725309270181)
XLA Ops:
  0.6 0.1 pad_add_fusion.place_ref
  0.7 0.0 copy-start
  0.7 1.1 %copy-done = bf16[1,1024,384]{2,1,0:T(8,128)(2,1)S(1)} copy-done((bf16[1,1024,384]{2,1,0:T(8,128)(2,1)S(1)}, bf16[1,1024,384]{2,1,0:T(8,128)(2,1)}, u32[]{:S(2)}) %copy-start) | copy-done | bytes 786456
  1.8 0.0 copy-start.1
  1.8 0.7 %copy-done.1 = s32[1,384]{1,0:T(1,128)S(1)} copy-done((s32[1,384]{1,0:T(1,128)S(1)}, s32[1,384]{1,0:T(1,128)}, u32[]{:S(2)}) %copy-start.1) | copy-done | bytes 1560
  2.5 1.8 %shard_map.50 = (bf16[1024,384]{1,0:T(8,128)(2,1)S(1)}, f32[328,128]{1,0:T(8,128)S(1)}, f32[328,128]{1,0:T(8,128)S(1)}) custom-call(s32[2]{0:T(128)S(1)} %pad_add_fusion.place_ref, s32[1,384]{1,0:T(1,128)S(1)} %copy-done.1, bf16[1024,384]{1,0:T(8,128)(2,1)S(1)} %bitcast.5), custom_call_target="tpu_custom_call" | custom-call | tf_op jit(solution)/shard_map/pallas_call | solution.py:267
  4.3 0.0 copy-start.2
  4.3 0.7 %copy-done.2 = s32[1,256]{1,0:T(1,128)S(1)} copy-done((s32[1,256]{1,0:T(1,128)S(1)}, s32[1,256]{1,0:T(1,128)}, u32[]{:S(2)}) %copy-start.2) | copy-done | bytes 1048
  5.0 1.0 %shard_map.51 = (f32[128,384]{1,0:T(8,128)S(1)}, f32[128,384]{1,0:T(8,128)S(1)}) custom-call(s32[2]{0:T(128)S(1)} %pad_add_fusion.place_ref, s32[1,256]{1,0:T(1,128)S(1)} %copy-done.2, bf16[1024,384]{1,0:T(8,128)(2,1)S(1)} %get-tuple-element.14.p_ref), custom_call_target="tpu_custom_call" | custom-call | tf_op jit(solution)/shard_map/pallas_call | solution.py:267
  6.0 3.1 %collective-permute-start = (f32[128,384]{1,0:T(8,128)S(1)}, f32[128,384]{1,0:T(8,128)S(1)}, u32[]{:S(2)}, u32[]{:S(2)}) collective-permute-start(f32[128,384]{1,0:T(8,128)S(1)} %get-tuple-element.16), channel_id=1, source_target_pairs={{0,1},{1,0},{2,3},{3,2},{4,5},{5,4},{6,7},{7,6},{8,9},{9,8},{10,11... | collective-permute-start | bytes 589832 | tf_op jit(solution)/shard_map/ppermute | solution.py:281
  9.2 0.1 collective-permute-start.3
  9.2 5.7 %collective-permute-done = f32[128,384]{1,0:T(8,128)S(1)} collective-permute-done((f32[128,384]{1,0:T(8,128)S(1)}, f32[128,384]{1,0:T(8,128)S(1)}, u32[]{:S(2)}, u32[]{:S(2)}) %collective-permute-start) | collective-permute-done | bytes 196640 | tf_op jit(solution)/shard_map/ppermute | solution.py:281
  14.9 4.1 %collective-permute-start.1 = (f32[128,384]{1,0:T(8,128)S(1)}, f32[128,384]{1,0:T(8,128)S(1)}, u32[]{:S(2)}, u32[]{:S(2)}) collective-permute-start(f32[128,384]{1,0:T(8,128)S(1)} %add.12), channel_id=1, source_target_pairs={{0,3},{1,2},{2,1},{3,0},{4,7},{5,6},{6,5},{7,4},{8,11},{9,10},{10,... | collective-permute-start | bytes 589832 | tf_op jit(solution)/shard_map/ppermute | solution.py:281
  19.0 0.0 collective-permute-done.3
  19.1 4.5 %collective-permute-start.4 = (f32[328,128]{1,0:T(8,128)S(1)}, f32[328,128]{1,0:T(8,128)S(1)}, u32[]{:S(2)}, u32[]{:S(2)}) collective-permute-start(f32[328,128]{1,0:T(8,128)S(1)} %add.14), channel_id=1, source_target_pairs={{0,3},{1,2},{2,1},{3,0},{4,7},{5,6},{6,5},{7,4},{8,11},{9,10},{10,... | collective-permute-start | bytes 503816 | tf_op jit(solution)/shard_map/ppermute | solution.py:281
  23.6 1.7 %collective-permute-done.1 = f32[128,384]{1,0:T(8,128)S(1)} collective-permute-done((f32[128,384]{1,0:T(8,128)S(1)}, f32[128,384]{1,0:T(8,128)S(1)}, u32[]{:S(2)}, u32[]{:S(2)}) %collective-permute-start.1) | collective-permute-done | bytes 196640 | tf_op jit(solution)/shard_map/ppermute | solution.py:281
  25.3 6.4 %collective-permute-start.2 = (f32[128,384]{1,0:T(8,128)S(1)}, f32[128,384]{1,0:T(8,128)S(1)}, u32[]{:S(2)}, u32[]{:S(2)}) collective-permute-start(f32[128,384]{1,0:T(8,128)S(1)} %add.13.mine_ref), channel_id=1, source_target_pairs={{0,1},{1,0},{2,3},{3,2},{4,5},{5,4},{6,7},{7,6},{8,9},{9,8},{10,11... | collective-permute-start | bytes 589832 | tf_op jit(solution)/shard_map/ppermute | solution.py:281
  31.7 0.0 collective-permute-done.4
  31.8 1.8 %collective-permute-start.5 = (f32[328,128]{1,0:T(8,128)S(1)}, f32[328,128]{1,0:T(8,128)S(1)}, u32[]{:S(2)}, u32[]{:S(2)}) collective-permute-start(f32[328,128]{1,0:T(8,128)S(1)} %add.15.mine_ref), channel_id=1, source_target_pairs={{0,1},{1,0},{2,3},{3,2},{4,5},{5,4},{6,7},{7,6},{8,9},{9,8},{10,11... | collective-permute-start | bytes 503816 | tf_op jit(solution)/shard_map/ppermute | solution.py:281
  33.5 4.8 %collective-permute-done.5.other_ref = f32[328,128]{1,0:T(8,128)S(1)} collective-permute-done((f32[328,128]{1,0:T(8,128)S(1)}, f32[328,128]{1,0:T(8,128)S(1)}, u32[]{:S(2)}, u32[]{:S(2)}) %collective-permute-start.5) | collective-permute-done | bytes 167968 | tf_op jit(solution)/shard_map/ppermute | solution.py:281
  38.3 7.3 %shard_map.52 = (f32[128,384]{1,0:T(8,128)S(1)}, f32[128,256]{1,0:T(8,128)S(1)}, f32[128,128]{1,0:T(8,128)S(1)}, f32[128,256]{1,0:T(8,128)S(1)}) custom-call(s32[2]{0:T(128)S(1)} %pad_add_fusion.place_ref, f32[328,128]{1,0:T(8,128)S(1)} %add.15.mine_ref, f32[328,128]{1,0:T(8,128)S(1)} %collective-permute-done.5.other_ref), custom_call_target="tpu_custom_call" | custom-call | tf_op jit(solution)/shard_map/pallas_call | solution.py:267
  45.7 4.7 %shard_map.53 = (f32[128,128]{1,0:T(8,128)}, f32[128,384]{1,0:T(8,128)S(1)}) custom-call(s32[2]{0:T(128)S(1)} %pad_add_fusion.place_ref, f32[328,128]{1,0:T(8,128)S(1)} %add.15.mine_ref, f32[328,128]{1,0:T(8,128)S(1)} %collective-permute-done.5.other_ref, f32[128,384]{1,0:T(8,128)S(1)} %get-tuple-element.21.refs_0_, ...), custom_call_target="tpu_custom_call" | custom-call | tf_op jit(solution)/shard_map/pallas_call | solution.py:267
  50.4 0.0 collective-permute-done.2.other_ref
  50.4 10.6 %shard_map.54 = (f32[1024,384]{1,0:T(8,128)}, bf16[1024,256]{1,0:T(8,128)(2,1)}) custom-call(s32[2]{0:T(128)S(1)} %pad_add_fusion.place_ref, bf16[1024,384]{1,0:T(8,128)(2,1)S(1)} %get-tuple-element.14.p_ref, f32[128,384]{1,0:T(8,128)S(1)} %add.13.mine_ref, f32[128,384]{1,0:T(8,128)S(1)} %collective-permute-done.2.other_ref, ...), custom_call_target="tpu_custom_call" | custom-call | tf_op jit(solution)/shard_map/pallas_call | solution.py:267
  (4 shorter events, 0.1 us)
Async XLA Ops:
  0.7 1.1 %copy-start = (bf16[1,1024,384]{2,1,0:T(8,128)(2,1)S(1)}, bf16[1,1024,384]{2,1,0:T(8,128)(2,1)}, u32[]{:S(2)}) copy-start(bf16[1,1024,384]{2,1,0:T(8,128)(2,1)} %param.3) | copy-start | bytes 2359300
  1.8 0.7 %copy-start.1 = (s32[1,384]{1,0:T(1,128)S(1)}, s32[1,384]{1,0:T(1,128)}, u32[]{:S(2)}) copy-start(s32[1,384]{1,0:T(1,128)} %order_ref.1) | copy-start | bytes 4612
  4.3 0.7 %copy-start.2 = (s32[1,256]{1,0:T(1,128)S(1)}, s32[1,256]{1,0:T(1,128)}, u32[]{:S(2)}) copy-start(s32[1,256]{1,0:T(1,128)} %skel_ref.1) | copy-start | bytes 3076
  6.0 8.9 %collective-permute-start = (f32[128,384]{1,0:T(8,128)S(1)}, f32[128,384]{1,0:T(8,128)S(1)}, u32[]{:S(2)}, u32[]{:S(2)}) collective-permute-start(f32[128,384]{1,0:T(8,128)S(1)} %get-tuple-element.16), channel_id=1, source_target_pairs={{0,1},{1,0},{2,3},{3,2},{4,5},{5,4},{6,7},{7,6},{8,9},{9,8},{10,11... | collective-permute-start | bytes 589832 | tf_op jit(solution)/shard_map/ppermute | solution.py:281
  9.2 9.9 %collective-permute-start.3 = (f32[328,128]{1,0:T(8,128)S(1)}, f32[328,128]{1,0:T(8,128)S(1)}, u32[]{:S(2)}, u32[]{:S(2)}) collective-permute-start(f32[328,128]{1,0:T(8,128)S(1)} %get-tuple-element.18), channel_id=1, source_target_pairs={{0,1},{1,0},{2,3},{3,2},{4,5},{5,4},{6,7},{7,6},{8,9},{9,8},{10,11... | collective-permute-start | bytes 503816 | tf_op jit(solution)/shard_map/ppermute | solution.py:281
  14.9 10.4 %collective-permute-start.1 = (f32[128,384]{1,0:T(8,128)S(1)}, f32[128,384]{1,0:T(8,128)S(1)}, u32[]{:S(2)}, u32[]{:S(2)}) collective-permute-start(f32[128,384]{1,0:T(8,128)S(1)} %add.12), channel_id=1, source_target_pairs={{0,3},{1,2},{2,1},{3,0},{4,7},{5,6},{6,5},{7,4},{8,11},{9,10},{10,... | collective-permute-start | bytes 589832 | tf_op jit(solution)/shard_map/ppermute | solution.py:281
  19.1 12.7 %collective-permute-start.4 = (f32[328,128]{1,0:T(8,128)S(1)}, f32[328,128]{1,0:T(8,128)S(1)}, u32[]{:S(2)}, u32[]{:S(2)}) collective-permute-start(f32[328,128]{1,0:T(8,128)S(1)} %add.14), channel_id=1, source_target_pairs={{0,3},{1,2},{2,1},{3,0},{4,7},{5,6},{6,5},{7,4},{8,11},{9,10},{10,... | collective-permute-start | bytes 503816 | tf_op jit(solution)/shard_map/ppermute | solution.py:281
  25.3 25.1 %collective-permute-start.2 = (f32[128,384]{1,0:T(8,128)S(1)}, f32[128,384]{1,0:T(8,128)S(1)}, u32[]{:S(2)}, u32[]{:S(2)}) collective-permute-start(f32[128,384]{1,0:T(8,128)S(1)} %add.13.mine_ref), channel_id=1, source_target_pairs={{0,1},{1,0},{2,3},{3,2},{4,5},{5,4},{6,7},{7,6},{8,9},{9,8},{10,11... | collective-permute-start | bytes 589832 | tf_op jit(solution)/shard_map/ppermute | solution.py:281
  31.8 6.6 %collective-permute-start.5 = (f32[328,128]{1,0:T(8,128)S(1)}, f32[328,128]{1,0:T(8,128)S(1)}, u32[]{:S(2)}, u32[]{:S(2)}) collective-permute-start(f32[328,128]{1,0:T(8,128)S(1)} %add.15.mine_ref), channel_id=1, source_target_pairs={{0,1},{1,0},{2,3},{3,2},{4,5},{5,4},{6,7},{7,6},{8,9},{9,8},{10,11... | collective-permute-start | bytes 503816 | tf_op jit(solution)/shard_map/ppermute | solution.py:281

commit v3 on v2

--- a/solution.py
+++ b/solution.py
@@ -43,29 +43,52 @@
     return jnp.broadcast_to(x[s : s + 1, :], (8, LANES))
 
 
-def factor_strip(tiles, lane):
-    diag = tiles[0]
-    cols = [
-        [jnp.broadcast_to(diag[g][:, lane + j : lane + j + 1], (8, LANES)) if g >= j // 8 else None for g in range(GROUPS)]
-        for j in range(STRIP)
+def spread(tile, lane, first, count):
+    return [
+        [
+            jnp.broadcast_to(tile[g][:, lane + first + j : lane + first + j + 1], (8, LANES)) if g >= first // 8 else None
+            for g in range(GROUPS)
+        ]
+        for j in range(count)
     ]
-    tiles = [list(t) for t in tiles]
+
+
+def eliminate(tile, sub, steps, first):
+    tile = list(tile)
+    for k, (inv, low) in enumerate(steps, first):
+        g0, s = divmod(k, 8)
+        row = row_of(tile[g0], s) * inv
+        below = jnp.where(sub > s, low[g0], 0.0)
+        tile[g0] = jnp.where(sub == s, row, tile[g0] - below * row)
+        for g in range(g0 + 1, GROUPS):
+            tile[g] = tile[g] - low[g] * row
+    return tile
+
+
+def factor_strip(diag, lane):
     sub = lax.broadcasted_iota(jnp.int32, (8, LANES), 0)
-    for k in range(STRIP):
-        g0, s = divmod(k, 8)
-        inv = lax.rsqrt(row_of(cols[k][g0], s))
-        low = [cols[k][g] * inv if g >= g0 else None for g in range(GROUPS)]
-        for j in range(k + 1, STRIP):
-            factor = row_of(low[j // 8], j % 8)
-            for g in range(j // 8, GROUPS):
-                cols[j][g] = cols[j][g] - low[g] * factor
-        below = jnp.where(sub > s, low[g0], 0.0)
-        for t in tiles:
-            row = row_of(t[g0], s) * inv
-            t[g0] = jnp.where(sub == s, row, t[g0] - below * row)
-            for g in range(g0 + 1, GROUPS):
-                t[g] = t[g] - low[g] * row
-    return tiles
+    now = spread(diag, lane, 0, 8)
+    steps = []
+    for first in range(0, STRIP, 8):
+        after = spread(diag, lane, first + 8, 8) if first + 8 < STRIP else []
+        done = []
+        for k in range(8):
+            g0 = first // 8
+            inv = lax.rsqrt(row_of(now[k][g0], k))
+            low = [now[k][g] * inv if g >= g0 else None for g in range(GROUPS)]
+            for j in range(k + 1, 8):
+                factor = row_of(low[g0], j)
+                for g in range(g0, GROUPS):
+                    now[j][g] = now[j][g] - low[g] * factor
+            for j in range(len(after)):
+                factor = row_of(low[g0 + 1], j)
+                for g in range(g0 + 1, GROUPS):
+                    after[j][g] = after[j][g] - low[g] * factor
+            done.append((inv, low))
+        diag = eliminate(diag, sub, done, first)
+        steps += done
+        now = after
+    return steps, diag, sub
 
 
 def block(i):
@@ -83,7 +106,7 @@
 
 def stack_left(x):
     high, low = split(x)
-    return [high, high, low]
+    return jnp.concatenate([high, high, low], axis=0).T
 
 
 def stack_right(x):
@@ -92,26 +115,32 @@
 
 
 def take_out(ref, rows, t, lefts, rights):
-    left = jnp.concatenate([part for x in lefts for part in x], axis=0)
+    left = lefts[0] if len(lefts) == 1 else jnp.concatenate(lefts, axis=1)
     right = jnp.concatenate([part for x in rights for part in stack_right(x)], axis=0)
-    ref[rows, block(t)] = ref[rows, block(t)] - dot(left, right, TN)
-
-
-def factor_panel(u_ref, t_ref):
+    ref[rows, block(t)] = ref[rows, block(t)] - dot(left, right, NN)
+
+
+def factor_panel(u_ref, t_ref, beside=None):
     targets = [(u_ref, t) for t in range(u_ref.shape[1] // LANES)]
     targets += [(t_ref, t) for t in range(t_ref.shape[1] // LANES)]
     for r0 in range(0, LANES, STRIP):
-        tiles = [[ref[r0 + 8 * g : r0 + 8 * g + 8, block(t)] for g in range(GROUPS)] for ref, t in targets]
-        tiles = factor_strip(tiles, r0)
-        for (ref, t), tile in zip(targets, tiles):
-            for g in range(GROUPS):
-                ref[r0 + 8 * g : r0 + 8 * g + 8, block(t)] = tile[g]
-        if r0 + STRIP < LANES:
-            rows = slice(r0 + STRIP, LANES)
-            whole = [jnp.concatenate(tile, axis=0) for tile in tiles]
-            left = stack_left(whole[0][:, r0 + STRIP :])
-            for (ref, t), right in zip(targets, whole):
-                take_out(ref, rows, t, [left], [right])
+        last = r0 + STRIP == LANES
+        rows = slice(r0 + STRIP, LANES)
+        steps = left = sub = None
+        if beside:
+            beside(r0 // STRIP)
+        for ref, t in targets:
+            tile = [ref[r0 + 8 * g : r0 + 8 * g + 8, block(t)] for g in range(GROUPS)]
+            if steps is None:
+                steps, tile, sub = factor_strip(tile, r0)
+            else:
+                tile = eliminate(tile, sub, steps, 0)
+            whole = jnp.concatenate(tile, axis=0)
+            ref[r0 : r0 + STRIP, block(t)] = whole
+            if not last:
+                if left is None:
+                    left = stack_left(whole)[r0 + STRIP :]
+                take_out(ref, rows, t, [left], [whole])
 
 
 def take_out_panels(u_before, t_before, u_ref, t_ref):
@@ -226,23 +255,38 @@
 
 
 def finish_kernel(place_ref, p_ref, mine_ref, other_ref, *refs):
-    t_parts = refs[:-5]
-    q_ref, w_ref, tt_ref, a_ref, s_ref = refs[-5:]
+    t_parts = refs[:-9]
+    q_out, w_out, tt_ref, a_ref, s_ref, q_ref, cross_ref, w_ref, sems = refs[-9:]
     even = place_ref[1] == 0
     k = a_ref.shape[0]
+    rows = p_ref.shape[0]
     for i, part in enumerate(t_parts):
         tt_ref[block(i), : part.shape[1]] = part[...]
         if i + 1 < len(t_parts):
             tt_ref[block(i), part.shape[1] :] = jnp.zeros((LANES, tt_ref.shape[1] - part.shape[1]), F32)
     t = tt_ref[...]
     y = join(even, mine_ref[...], other_ref[...]).astype(BF16)
-    p = p_ref[...]
     qskel = exact_left(y, t, NT)
     a_ref[...] = product(qskel, qskel, NT)
-    q = exact_left(p, t, NT)
-    q_ref[...] = q
-    cross = product(q, qskel, NT)
     panels = k // LANES
+    per = LANES // STRIP
+    pieces = panels * per
+    piece = rows // pieces
+    copies = []
+
+    def write(src, dst, i, sem):
+        at = pl.ds(piece * i, piece)
+        copies.append(pltpu.make_async_copy(src.at[at], dst.at[at], sem))
+        copies[-1].start()
+
+    def beside(i):
+        if i:
+            write(q_ref, q_out, i - 1, sems.at[0, i - 1])
+        at = slice(piece * i, piece * (i + 1))
+        q = exact_left(p_ref[at], t, NT)
+        q_ref[at] = q
+        cross_ref[at] = product(q, qskel, NT)
+
     us = [a_ref.at[block(i), LANES * i :] for i in range(panels)]
     ts = [s_ref.at[block(i), : LANES * (i + 1)] for i in range(panels)]
     for i in range(panels):
@@ -250,10 +294,18 @@
         if i + 1 < panels:
             s_ref[block(i), LANES * (i + 1) :] = jnp.zeros((LANES, k - LANES * (i + 1)), F32)
         take_out_panels(us[:i], ts[:i], us[i], ts[i])
-        factor_panel(us[i], ts[i])
+        factor_panel(us[i], ts[i], lambda strip, i=i: beside(per * i + strip))
+    write(q_ref, q_out, pieces - 1, sems.at[0, pieces - 1])
     s = s_ref[...]
     inverse = product(s, s, TN)
-    w_ref[...] = product(cross, inverse, NN).astype(BF16)
+    for i in range(pieces):
+        at = slice(piece * i, piece * (i + 1))
+        w_ref[at] = product(cross_ref[at], inverse, NN).astype(BF16)
+        if i:
+            write(w_ref, w_out, i - 1, sems.at[1, i - 1])
+    write(w_ref, w_out, pieces - 1, sems.at[1, pieces - 1])
+    for copy in copies:
+        copy.wait()
 
 
 def vmem(shape, dtype):
@@ -263,13 +315,14 @@
 PARAMS = pltpu.CompilerParams(vmem_limit_bytes=48 * 1024 * 1024)
 
 
-def call(kernel, out_shape, place, *args, scratch=()):
+def call(kernel, out_shape, place, *args, scratch=(), **kwargs):
     return pl.pallas_call(
         kernel,
         in_specs=[pl.BlockSpec(memory_space=pltpu.SMEM)] + [pl.BlockSpec()] * len(args),
         out_shape=out_shape,
         scratch_shapes=scratch,
         compiler_params=PARAMS,
+        **kwargs,
     )(place, *args)
 
 
@@ -344,7 +397,16 @@
             mine_y,
             other_y,
             *ts,
-            scratch=[vmem((c, c), F32), vmem((k, k), F32), vmem((k, k), F32)],
+            scratch=[
+                vmem((c, c), F32),
+                vmem((k, k), F32),
+                vmem((k, k), F32),
+                vmem((rows, c), F32),
+                vmem((rows, k), F32),
+                vmem((rows, k), BF16),
+                pltpu.SemaphoreType.DMA((2, k // STRIP)),
+            ],
+            out_specs=(pl.BlockSpec(memory_space=pl.ANY),) * 2,
         )
         q_all.append(q)
         w_all.append(w)

time: 61.2 us -> 58.2 us (0.951)
  Pallas kernels: 25.5 us -> 22.3 us
    pallas_call x5, Pallas kernels: 25.5 us -> 22.3 us  [call(): pl.pallas_call(kernel, in_specs=[pl.BlockSpec(memory_space=pltpu.SMEM)] +...]
  transfers between devices with their start and end apart: 6 -> 6, of which waited for: 3 -> 3; matrix products, arithmetic and copies ran while one was open for 0% -> 0% of each run, Pallas kernels for 20% -> 18%
where the time goes in v3:
time: 58.2 us; the launch traced here: 58 us
  Pallas kernels  22.3 us (38%)
  starting transfers between devices  20 us (34%)
  waiting for transfers between devices  12.2 us (21%)
  local copies, waits for them, and re-layouts  2.49 us (4%)
  between operations  0.85 us (1%)
    pallas_call x5, Pallas kernels, call(): pl.pallas_call(kernel, in_specs=[pl.BlockSpec(memory_space=pltpu.SMEM)] +...  22.3 us
    ppermute x6, starting transfers between devices, swap(): return lax.ppermute(x, 'row', pairs)  20 us
    ppermute x6, waiting for transfers between devices, swap(): return lax.ppermute(x, 'row', pairs)  12.2 us
    unnamed x6, local copies, waits for them, and re-layouts  2.49 us
  transfers between devices with their start and end apart: 6, of which 3 were waited for; matrix products, arithmetic and copies ran while one was open for 0% of the time, Pallas kernels for 18%

profile of v3, /device:TPU:0, one launch (start us, length us, event | category | flops | bytes accessed | tf_op | source)
XLA Modules:
  0.0 58.0 jit_solution(4129952259327174824)
XLA Ops:
  0.6 0.1 pad_add_fusion.place_ref
  0.7 0.0 copy-start
  0.7 1.1 %copy-done = bf16[1,1024,384]{2,1,0:T(8,128)(2,1)S(1)} copy-done((bf16[1,1024,384]{2,1,0:T(8,128)(2,1)S(1)}, bf16[1,1024,384]{2,1,0:T(8,128)(2,1)}, u32[]{:S(2)}) %copy-start) | copy-done | bytes 786456
  1.8 0.0 copy-start.1
  1.8 0.7 %copy-done.1 = s32[1,384]{1,0:T(1,128)S(1)} copy-done((s32[1,384]{1,0:T(1,128)S(1)}, s32[1,384]{1,0:T(1,128)}, u32[]{:S(2)}) %copy-start.1) | copy-done | bytes 1560
  2.5 1.8 %shard_map.50 = (bf16[1024,384]{1,0:T(8,128)(2,1)S(1)}, f32[328,128]{1,0:T(8,128)S(1)}, f32[328,128]{1,0:T(8,128)S(1)}) custom-call(s32[2]{0:T(128)S(1)} %pad_add_fusion.place_ref, s32[1,384]{1,0:T(1,128)S(1)} %copy-done.1, bf16[1024,384]{1,0:T(8,128)(2,1)S(1)} %bitcast.5), custom_call_target="tpu_custom_call" | custom-call | tf_op jit(solution)/shard_map/pallas_call | solution.py:319
  4.3 0.0 copy-start.2
  4.3 0.7 %copy-done.2 = s32[1,256]{1,0:T(1,128)S(1)} copy-done((s32[1,256]{1,0:T(1,128)S(1)}, s32[1,256]{1,0:T(1,128)}, u32[]{:S(2)}) %copy-start.2) | copy-done | bytes 1048
  5.0 1.0 %shard_map.51 = (f32[128,384]{1,0:T(8,128)S(1)}, f32[128,384]{1,0:T(8,128)S(1)}) custom-call(s32[2]{0:T(128)S(1)} %pad_add_fusion.place_ref, s32[1,256]{1,0:T(1,128)S(1)} %copy-done.2, bf16[1024,384]{1,0:T(8,128)(2,1)S(1)} %get-tuple-element.14.p_ref), custom_call_target="tpu_custom_call" | custom-call | tf_op jit(solution)/shard_map/pallas_call | solution.py:319
  6.0 3.1 %collective-permute-start = (f32[128,384]{1,0:T(8,128)S(1)}, f32[128,384]{1,0:T(8,128)S(1)}, u32[]{:S(2)}, u32[]{:S(2)}) collective-permute-start(f32[128,384]{1,0:T(8,128)S(1)} %get-tuple-element.16), channel_id=1, source_target_pairs={{0,1},{1,0},{2,3},{3,2},{4,5},{5,4},{6,7},{7,6},{8,9},{9,8},{10,11... | collective-permute-start | bytes 589832 | tf_op jit(solution)/shard_map/ppermute | solution.py:334
  9.2 0.1 collective-permute-start.3
  9.2 5.7 %collective-permute-done = f32[128,384]{1,0:T(8,128)S(1)} collective-permute-done((f32[128,384]{1,0:T(8,128)S(1)}, f32[128,384]{1,0:T(8,128)S(1)}, u32[]{:S(2)}, u32[]{:S(2)}) %collective-permute-start) | collective-permute-done | bytes 196640 | tf_op jit(solution)/shard_map/ppermute | solution.py:334
  14.9 4.1 %collective-permute-start.1 = (f32[128,384]{1,0:T(8,128)S(1)}, f32[128,384]{1,0:T(8,128)S(1)}, u32[]{:S(2)}, u32[]{:S(2)}) collective-permute-start(f32[128,384]{1,0:T(8,128)S(1)} %add.12), channel_id=1, source_target_pairs={{0,3},{1,2},{2,1},{3,0},{4,7},{5,6},{6,5},{7,4},{8,11},{9,10},{10,... | collective-permute-start | bytes 589832 | tf_op jit(solution)/shard_map/ppermute | solution.py:334
  19.0 0.0 collective-permute-done.3
  19.1 4.5 %collective-permute-start.4 = (f32[328,128]{1,0:T(8,128)S(1)}, f32[328,128]{1,0:T(8,128)S(1)}, u32[]{:S(2)}, u32[]{:S(2)}) collective-permute-start(f32[328,128]{1,0:T(8,128)S(1)} %add.14), channel_id=1, source_target_pairs={{0,3},{1,2},{2,1},{3,0},{4,7},{5,6},{6,5},{7,4},{8,11},{9,10},{10,... | collective-permute-start | bytes 503816 | tf_op jit(solution)/shard_map/ppermute | solution.py:334
  23.6 1.7 %collective-permute-done.1 = f32[128,384]{1,0:T(8,128)S(1)} collective-permute-done((f32[128,384]{1,0:T(8,128)S(1)}, f32[128,384]{1,0:T(8,128)S(1)}, u32[]{:S(2)}, u32[]{:S(2)}) %collective-permute-start.1) | collective-permute-done | bytes 196640 | tf_op jit(solution)/shard_map/ppermute | solution.py:334
  25.3 6.4 %collective-permute-start.2 = (f32[128,384]{1,0:T(8,128)S(1)}, f32[128,384]{1,0:T(8,128)S(1)}, u32[]{:S(2)}, u32[]{:S(2)}) collective-permute-start(f32[128,384]{1,0:T(8,128)S(1)} %add.13.mine_ref), channel_id=1, source_target_pairs={{0,1},{1,0},{2,3},{3,2},{4,5},{5,4},{6,7},{7,6},{8,9},{9,8},{10,11... | collective-permute-start | bytes 589832 | tf_op jit(solution)/shard_map/ppermute | solution.py:334
  31.7 0.0 collective-permute-done.4
  31.8 1.8 %collective-permute-start.5 = (f32[328,128]{1,0:T(8,128)S(1)}, f32[328,128]{1,0:T(8,128)S(1)}, u32[]{:S(2)}, u32[]{:S(2)}) collective-permute-start(f32[328,128]{1,0:T(8,128)S(1)} %add.15.mine_ref), channel_id=1, source_target_pairs={{0,1},{1,0},{2,3},{3,2},{4,5},{5,4},{6,7},{7,6},{8,9},{9,8},{10,11... | collective-permute-start | bytes 503816 | tf_op jit(solution)/shard_map/ppermute | solution.py:334
  33.5 4.8 %collective-permute-done.5.other_ref = f32[328,128]{1,0:T(8,128)S(1)} collective-permute-done((f32[328,128]{1,0:T(8,128)S(1)}, f32[328,128]{1,0:T(8,128)S(1)}, u32[]{:S(2)}, u32[]{:S(2)}) %collective-permute-start.5) | collective-permute-done | bytes 167968 | tf_op jit(solution)/shard_map/ppermute | solution.py:334
  38.3 6.2 %shard_map.52 = (f32[128,384]{1,0:T(8,128)S(1)}, f32[128,256]{1,0:T(8,128)S(1)}, f32[128,128]{1,0:T(8,128)S(1)}, f32[128,256]{1,0:T(8,128)S(1)}) custom-call(s32[2]{0:T(128)S(1)} %pad_add_fusion.place_ref, f32[328,128]{1,0:T(8,128)S(1)} %add.15.mine_ref, f32[328,128]{1,0:T(8,128)S(1)} %collective-permute-done.5.other_ref), custom_call_target="tpu_custom_call" | custom-call | tf_op jit(solution)/shard_map/pallas_call | solution.py:319
  44.5 4.1 %shard_map.53 = (f32[128,128]{1,0:T(8,128)}, f32[128,384]{1,0:T(8,128)S(1)}) custom-call(s32[2]{0:T(128)S(1)} %pad_add_fusion.place_ref, f32[328,128]{1,0:T(8,128)S(1)} %add.15.mine_ref, f32[328,128]{1,0:T(8,128)S(1)} %collective-permute-done.5.other_ref, f32[128,384]{1,0:T(8,128)S(1)} %get-tuple-element.21.refs_0_, ...), custom_call_target="tpu_custom_call" | custom-call | tf_op jit(solution)/shard_map/pallas_call | solution.py:319
  48.6 0.0 collective-permute-done.2.other_ref
  48.6 9.2 %shard_map.54 = (f32[1024,384]{1,0:T(8,128)}, bf16[1024,256]{1,0:T(8,128)(2,1)}) custom-call(s32[2]{0:T(128)S(1)} %pad_add_fusion.place_ref, bf16[1024,384]{1,0:T(8,128)(2,1)S(1)} %get-tuple-element.14.p_ref, f32[128,384]{1,0:T(8,128)S(1)} %add.13.mine_ref, f32[128,384]{1,0:T(8,128)S(1)} %collective-permute-done.2.other_ref, ...), custom_call_target="tpu_custom_call" | custom-call | tf_op jit(solution)/shard_map/pallas_call | solution.py:319
  (4 shorter events, 0.1 us)
Async XLA Ops:
  0.7 1.1 %copy-start = (bf16[1,1024,384]{2,1,0:T(8,128)(2,1)S(1)}, bf16[1,1024,384]{2,1,0:T(8,128)(2,1)}, u32[]{:S(2)}) copy-start(bf16[1,1024,384]{2,1,0:T(8,128)(2,1)} %param.3) | copy-start | bytes 2359300
  1.8 0.7 %copy-start.1 = (s32[1,384]{1,0:T(1,128)S(1)}, s32[1,384]{1,0:T(1,128)}, u32[]{:S(2)}) copy-start(s32[1,384]{1,0:T(1,128)} %order_ref.1) | copy-start | bytes 4612
  4.3 0.7 %copy-start.2 = (s32[1,256]{1,0:T(1,128)S(1)}, s32[1,256]{1,0:T(1,128)}, u32[]{:S(2)}) copy-start(s32[1,256]{1,0:T(1,128)} %skel_ref.1) | copy-start | bytes 3076
  6.0 8.9 %collective-permute-start = (f32[128,384]{1,0:T(8,128)S(1)}, f32[128,384]{1,0:T(8,128)S(1)}, u32[]{:S(2)}, u32[]{:S(2)}) collective-permute-start(f32[128,384]{1,0:T(8,128)S(1)} %get-tuple-element.16), channel_id=1, source_target_pairs={{0,1},{1,0},{2,3},{3,2},{4,5},{5,4},{6,7},{7,6},{8,9},{9,8},{10,11... | collective-permute-start | bytes 589832 | tf_op jit(solution)/shard_map/ppermute | solution.py:334
  9.2 9.9 %collective-permute-start.3 = (f32[328,128]{1,0:T(8,128)S(1)}, f32[328,128]{1,0:T(8,128)S(1)}, u32[]{:S(2)}, u32[]{:S(2)}) collective-permute-start(f32[328,128]{1,0:T(8,128)S(1)} %get-tuple-element.18), channel_id=1, source_target_pairs={{0,1},{1,0},{2,3},{3,2},{4,5},{5,4},{6,7},{7,6},{8,9},{9,8},{10,11... | collective-permute-start | bytes 503816 | tf_op jit(solution)/shard_map/ppermute | solution.py:334
  14.9 10.4 %collective-permute-start.1 = (f32[128,384]{1,0:T(8,128)S(1)}, f32[128,384]{1,0:T(8,128)S(1)}, u32[]{:S(2)}, u32[]{:S(2)}) collective-permute-start(f32[128,384]{1,0:T(8,128)S(1)} %add.12), channel_id=1, source_target_pairs={{0,3},{1,2},{2,1},{3,0},{4,7},{5,6},{6,5},{7,4},{8,11},{9,10},{10,... | collective-permute-start | bytes 589832 | tf_op jit(solution)/shard_map/ppermute | solution.py:334
  19.1 12.7 %collective-permute-start.4 = (f32[328,128]{1,0:T(8,128)S(1)}, f32[328,128]{1,0:T(8,128)S(1)}, u32[]{:S(2)}, u32[]{:S(2)}) collective-permute-start(f32[328,128]{1,0:T(8,128)S(1)} %add.14), channel_id=1, source_target_pairs={{0,3},{1,2},{2,1},{3,0},{4,7},{5,6},{6,5},{7,4},{8,11},{9,10},{10,... | collective-permute-start | bytes 503816 | tf_op jit(solution)/shard_map/ppermute | solution.py:334
  25.3 23.3 %collective-permute-start.2 = (f32[128,384]{1,0:T(8,128)S(1)}, f32[128,384]{1,0:T(8,128)S(1)}, u32[]{:S(2)}, u32[]{:S(2)}) collective-permute-start(f32[128,384]{1,0:T(8,128)S(1)} %add.13.mine_ref), channel_id=1, source_target_pairs={{0,1},{1,0},{2,3},{3,2},{4,5},{5,4},{6,7},{7,6},{8,9},{9,8},{10,11... | collective-permute-start | bytes 589832 | tf_op jit(solution)/shard_map/ppermute | solution.py:334
  31.8 6.6 %collective-permute-start.5 = (f32[328,128]{1,0:T(8,128)S(1)}, f32[328,128]{1,0:T(8,128)S(1)}, u32[]{:S(2)}, u32[]{:S(2)}) collective-permute-start(f32[328,128]{1,0:T(8,128)S(1)} %add.15.mine_ref), channel_id=1, source_target_pairs={{0,1},{1,0},{2,3},{3,2},{4,5},{5,4},{6,7},{7,6},{8,9},{9,8},{10,11... | collective-permute-start | bytes 503816 | tf_op jit(solution)/shard_map/ppermute | solution.py:334

commit v4 on v3

--- a/solution.py
+++ b/solution.py
@@ -162,12 +162,33 @@
 PACKED_ROWS = LANES // 2
 
 
+FOLDED_ROWS = 3 * LANES // 8
+
+
 def pack_list(count):
-    return [(i, j) for i, j in upper_blocks(0, count) if i != j or i > 1]
+    out, at = [], PACKED_ROWS
+    for i, j in upper_blocks(0, count):
+        if i != j or i > 1:
+            out.append((i, j, at, FOLDED_ROWS if i == j else PACKED_ROWS))
+            at += out[-1][-1]
+    return out
 
 
 def message_rows(count):
-    return PACKED_ROWS * (1 + len(pack_list(count))) + 8
+    return pack_list(count)[-1][2] + pack_list(count)[-1][3] + 8
+
+
+def fold(g):
+    half, quarter = LANES // 2, LANES // 4
+    right = lax.broadcasted_iota(jnp.int32, (quarter, LANES), 1) >= half
+    low = jnp.where(right, g[half : half + quarter], pltpu.roll(g[half + quarter :], half, 1))
+    return jnp.concatenate([g[:half], low], axis=0)
+
+
+def unfold(g):
+    half = LANES // 2
+    low = g[half:]
+    return jnp.concatenate([g[:half], low, pltpu.roll(low, half, 1)], axis=0)
 
 
 def masks():
@@ -186,40 +207,37 @@
     even = place_ref[1] == 0
     row_ids, col_ids = masks()
 
-    def put(at, g):
-        top, low = g[:PACKED_ROWS], g[PACKED_ROWS:]
-        keep_ref[PACKED_ROWS * at : PACKED_ROWS * (at + 1)] = jnp.where(even, top, low)
-        send_ref[PACKED_ROWS * at : PACKED_ROWS * (at + 1)] = jnp.where(even, low, top)
+    def put(at, size, g):
+        top, low = g[:size], g[size:]
+        keep_ref[at : at + size] = jnp.where(even, top, low)
+        send_ref[at : at + size] = jnp.where(even, low, top)
 
     d0 = dot(p[:, block(0)], p[:, block(0)], TN)
     d1 = dot(p[:, block(1)], p[:, block(1)], TN)
-    put(0, jnp.where(row_ids >= col_ids, d0, d1))
+    put(0, PACKED_ROWS, jnp.where(row_ids >= col_ids, d0, d1))
     diagonal = jnp.sum(jnp.where(row_ids == col_ids, d1, 0.0), axis=0, keepdims=True)
     diagonal = jnp.broadcast_to(diagonal, (8, LANES))
     for ref in (keep_ref, send_ref):
         ref[ref.shape[0] - 8 :] = diagonal
-    for at, (i, j) in enumerate(pack_list(count)):
-        put(at + 1, dot(p[:, block(i)], p[:, block(j)], TN))
+    for i, j, at, size in pack_list(count):
+        g = dot(p[:, block(i)], p[:, block(j)], TN)
+        put(at, size, fold(g) if i == j else g)
 
 
 def unpack(even, mine_ref, other_ref, count, scale):
-    def take(at):
-        return join(
-            even,
-            mine_ref[PACKED_ROWS * at : PACKED_ROWS * (at + 1)],
-            other_ref[PACKED_ROWS * at : PACKED_ROWS * (at + 1)],
-        ) * scale
+    def take(at, size):
+        return join(even, mine_ref[at : at + size], other_ref[at : at + size]) * scale
 
     row_ids, col_ids = masks()
-    shared = take(0)
+    shared = take(0, PACKED_ROWS)
     turned = shared.T
     diagonal = mine_ref[mine_ref.shape[0] - 8 :][0:1] * scale
     out = {
         (0, 0): jnp.where(row_ids >= col_ids, shared, turned),
         (1, 1): jnp.where(row_ids < col_ids, shared, jnp.where(row_ids > col_ids, turned, diagonal)),
     }
-    for at, spot in enumerate(pack_list(count)):
-        out[spot] = take(at + 1)
+    for i, j, at, size in pack_list(count):
+        out[i, j] = unfold(take(at, size)) if i == j else take(at, size)
     return out
 
 

time: 58.2 us -> 57.6 us (0.990)
  starting transfers between devices: 20 us -> 17.5 us
  waiting for transfers between devices: 12.2 us -> 14 us
    ppermute x6, starting transfers between devices: 20 us -> 17.5 us  [swap(): return lax.ppermute(x, 'row', pairs)]
    ppermute x6, waiting for transfers between devices: 12.2 us -> 14 us  [swap(): return lax.ppermute(x, 'row', pairs)]
where the time goes in v4:
time: 57.6 us; the launch traced here: 57.4 us
  Pallas kernels  22.4 us (39%)
  starting transfers between devices  17.5 us (30%)
  waiting for transfers between devices  14 us (24%)
  local copies, waits for them, and re-layouts  2.49 us (4%)
  between operations  0.84 us (1%)
    pallas_call x5, Pallas kernels, call(): pl.pallas_call(kernel, in_specs=[pl.BlockSpec(memory_space=pltpu.SMEM)] +...  22.4 us
    ppermute x6, starting transfers between devices, swap(): return lax.ppermute(x, 'row', pairs)  17.5 us
    ppermute x6, waiting for transfers between devices, swap(): return lax.ppermute(x, 'row', pairs)  14 us
    unnamed x6, local copies, waits for them, and re-layouts  2.49 us
  transfers between devices with their start and end apart: 6, of which 3 were waited for; matrix products, arithmetic and copies ran while one was open for 0% of the time, Pallas kernels for 18%

profile of v4, /device:TPU:0, one launch (start us, length us, event | category | flops | bytes accessed | tf_op | source)
XLA Modules:
  0.0 57.4 jit_solution(10261023917925571390)
XLA Ops:
  0.6 0.1 pad_add_fusion.place_ref
  0.7 0.0 copy-start
  0.7 1.1 %copy-done = bf16[1,1024,384]{2,1,0:T(8,128)(2,1)S(1)} copy-done((bf16[1,1024,384]{2,1,0:T(8,128)(2,1)S(1)}, bf16[1,1024,384]{2,1,0:T(8,128)(2,1)}, u32[]{:S(2)}) %copy-start) | copy-done | bytes 786456
  1.8 0.0 copy-start.1
  1.8 0.7 %copy-done.1 = s32[1,384]{1,0:T(1,128)S(1)} copy-done((s32[1,384]{1,0:T(1,128)S(1)}, s32[1,384]{1,0:T(1,128)}, u32[]{:S(2)}) %copy-start.1) | copy-done | bytes 1560
  2.5 1.9 %shard_map.50 = (bf16[1024,384]{1,0:T(8,128)(2,1)S(1)}, f32[312,128]{1,0:T(8,128)S(1)}, f32[312,128]{1,0:T(8,128)S(1)}) custom-call(s32[2]{0:T(128)S(1)} %pad_add_fusion.place_ref, s32[1,384]{1,0:T(1,128)S(1)} %copy-done.1, bf16[1024,384]{1,0:T(8,128)(2,1)S(1)} %bitcast.5), custom_call_target="tpu_custom_call" | custom-call | tf_op jit(solution)/shard_map/pallas_call | solution.py:337
  4.4 0.0 copy-start.2
  4.4 0.7 %copy-done.2 = s32[1,256]{1,0:T(1,128)S(1)} copy-done((s32[1,256]{1,0:T(1,128)S(1)}, s32[1,256]{1,0:T(1,128)}, u32[]{:S(2)}) %copy-start.2) | copy-done | bytes 1048
  5.1 1.0 %shard_map.51 = (f32[128,384]{1,0:T(8,128)S(1)}, f32[128,384]{1,0:T(8,128)S(1)}) custom-call(s32[2]{0:T(128)S(1)} %pad_add_fusion.place_ref, s32[1,256]{1,0:T(1,128)S(1)} %copy-done.2, bf16[1024,384]{1,0:T(8,128)(2,1)S(1)} %get-tuple-element.14.p_ref), custom_call_target="tpu_custom_call" | custom-call | tf_op jit(solution)/shard_map/pallas_call | solution.py:337
  6.1 3.1 %collective-permute-start = (f32[128,384]{1,0:T(8,128)S(1)}, f32[128,384]{1,0:T(8,128)S(1)}, u32[]{:S(2)}, u32[]{:S(2)}) collective-permute-start(f32[128,384]{1,0:T(8,128)S(1)} %get-tuple-element.16), channel_id=1, source_target_pairs={{0,1},{1,0},{2,3},{3,2},{4,5},{5,4},{6,7},{7,6},{8,9},{9,8},{10,11... | collective-permute-start | bytes 589832 | tf_op jit(solution)/shard_map/ppermute | solution.py:352
  9.2 0.1 collective-permute-start.3
  9.3 5.7 %collective-permute-done = f32[128,384]{1,0:T(8,128)S(1)} collective-permute-done((f32[128,384]{1,0:T(8,128)S(1)}, f32[128,384]{1,0:T(8,128)S(1)}, u32[]{:S(2)}, u32[]{:S(2)}) %collective-permute-start) | collective-permute-done | bytes 196640 | tf_op jit(solution)/shard_map/ppermute | solution.py:352
  15.0 4.1 %collective-permute-start.1 = (f32[128,384]{1,0:T(8,128)S(1)}, f32[128,384]{1,0:T(8,128)S(1)}, u32[]{:S(2)}, u32[]{:S(2)}) collective-permute-start(f32[128,384]{1,0:T(8,128)S(1)} %add.12), channel_id=1, source_target_pairs={{0,3},{1,2},{2,1},{3,0},{4,7},{5,6},{6,5},{7,4},{8,11},{9,10},{10,... | collective-permute-start | bytes 589832 | tf_op jit(solution)/shard_map/ppermute | solution.py:352
  19.1 0.0 collective-permute-done.3
  19.1 2.3 %collective-permute-start.4 = (f32[312,128]{1,0:T(8,128)S(1)}, f32[312,128]{1,0:T(8,128)S(1)}, u32[]{:S(2)}, u32[]{:S(2)}) collective-permute-start(f32[312,128]{1,0:T(8,128)S(1)} %add.14), channel_id=1, source_target_pairs={{0,3},{1,2},{2,1},{3,0},{4,7},{5,6},{6,5},{7,4},{8,11},{9,10},{10,... | collective-permute-start | bytes 479240 | tf_op jit(solution)/shard_map/ppermute | solution.py:352
  21.4 3.8 %collective-permute-done.1 = f32[128,384]{1,0:T(8,128)S(1)} collective-permute-done((f32[128,384]{1,0:T(8,128)S(1)}, f32[128,384]{1,0:T(8,128)S(1)}, u32[]{:S(2)}, u32[]{:S(2)}) %collective-permute-start.1) | collective-permute-done | bytes 196640 | tf_op jit(solution)/shard_map/ppermute | solution.py:352
  25.2 6.2 %collective-permute-start.2 = (f32[128,384]{1,0:T(8,128)S(1)}, f32[128,384]{1,0:T(8,128)S(1)}, u32[]{:S(2)}, u32[]{:S(2)}) collective-permute-start(f32[128,384]{1,0:T(8,128)S(1)} %add.13.mine_ref), channel_id=1, source_target_pairs={{0,1},{1,0},{2,3},{3,2},{4,5},{5,4},{6,7},{7,6},{8,9},{9,8},{10,11... | collective-permute-start | bytes 589832 | tf_op jit(solution)/shard_map/ppermute | solution.py:352
  31.5 0.0 collective-permute-done.4
  31.5 1.7 %collective-permute-start.5 = (f32[312,128]{1,0:T(8,128)S(1)}, f32[312,128]{1,0:T(8,128)S(1)}, u32[]{:S(2)}, u32[]{:S(2)}) collective-permute-start(f32[312,128]{1,0:T(8,128)S(1)} %add.15.mine_ref), channel_id=1, source_target_pairs={{0,1},{1,0},{2,3},{3,2},{4,5},{5,4},{6,7},{7,6},{8,9},{9,8},{10,11... | collective-permute-start | bytes 479240 | tf_op jit(solution)/shard_map/ppermute | solution.py:352
  33.2 4.5 %collective-permute-done.5.other_ref = f32[312,128]{1,0:T(8,128)S(1)} collective-permute-done((f32[312,128]{1,0:T(8,128)S(1)}, f32[312,128]{1,0:T(8,128)S(1)}, u32[]{:S(2)}, u32[]{:S(2)}) %collective-permute-start.5) | collective-permute-done | bytes 159776 | tf_op jit(solution)/shard_map/ppermute | solution.py:352
  37.7 6.2 %shard_map.52 = (f32[128,384]{1,0:T(8,128)S(1)}, f32[128,256]{1,0:T(8,128)S(1)}, f32[128,128]{1,0:T(8,128)S(1)}, f32[128,256]{1,0:T(8,128)S(1)}) custom-call(s32[2]{0:T(128)S(1)} %pad_add_fusion.place_ref, f32[312,128]{1,0:T(8,128)S(1)} %add.15.mine_ref, f32[312,128]{1,0:T(8,128)S(1)} %collective-permute-done.5.other_ref), custom_call_target="tpu_custom_call" | custom-call | tf_op jit(solution)/shard_map/pallas_call | solution.py:337
  43.9 4.1 %shard_map.53 = (f32[128,128]{1,0:T(8,128)}, f32[128,384]{1,0:T(8,128)S(1)}) custom-call(s32[2]{0:T(128)S(1)} %pad_add_fusion.place_ref, f32[312,128]{1,0:T(8,128)S(1)} %add.15.mine_ref, f32[312,128]{1,0:T(8,128)S(1)} %collective-permute-done.5.other_ref, f32[128,384]{1,0:T(8,128)S(1)} %get-tuple-element.21.refs_0_, ...), custom_call_target="tpu_custom_call" | custom-call | tf_op jit(solution)/shard_map/pallas_call | solution.py:337
  48.0 0.0 collective-permute-done.2.other_ref
  48.0 9.3 %shard_map.54 = (f32[1024,384]{1,0:T(8,128)}, bf16[1024,256]{1,0:T(8,128)(2,1)}) custom-call(s32[2]{0:T(128)S(1)} %pad_add_fusion.place_ref, bf16[1024,384]{1,0:T(8,128)(2,1)S(1)} %get-tuple-element.14.p_ref, f32[128,384]{1,0:T(8,128)S(1)} %add.13.mine_ref, f32[128,384]{1,0:T(8,128)S(1)} %collective-permute-done.2.other_ref, ...), custom_call_target="tpu_custom_call" | custom-call | tf_op jit(solution)/shard_map/pallas_call | solution.py:337
  (4 shorter events, 0.1 us)
Async XLA Ops:
  0.7 1.1 %copy-start = (bf16[1,1024,384]{2,1,0:T(8,128)(2,1)S(1)}, bf16[1,1024,384]{2,1,0:T(8,128)(2,1)}, u32[]{:S(2)}) copy-start(bf16[1,1024,384]{2,1,0:T(8,128)(2,1)} %param.3) | copy-start | bytes 2359300
  1.8 0.7 %copy-start.1 = (s32[1,384]{1,0:T(1,128)S(1)}, s32[1,384]{1,0:T(1,128)}, u32[]{:S(2)}) copy-start(s32[1,384]{1,0:T(1,128)} %order_ref.1) | copy-start | bytes 4612
  4.4 0.7 %copy-start.2 = (s32[1,256]{1,0:T(1,128)S(1)}, s32[1,256]{1,0:T(1,128)}, u32[]{:S(2)}) copy-start(s32[1,256]{1,0:T(1,128)} %skel_ref.1) | copy-start | bytes 3076
  6.1 8.9 %collective-permute-start = (f32[128,384]{1,0:T(8,128)S(1)}, f32[128,384]{1,0:T(8,128)S(1)}, u32[]{:S(2)}, u32[]{:S(2)}) collective-permute-start(f32[128,384]{1,0:T(8,128)S(1)} %get-tuple-element.16), channel_id=1, source_target_pairs={{0,1},{1,0},{2,3},{3,2},{4,5},{5,4},{6,7},{7,6},{8,9},{9,8},{10,11... | collective-permute-start | bytes 589832 | tf_op jit(solution)/shard_map/ppermute | solution.py:352
  9.2 9.9 %collective-permute-start.3 = (f32[312,128]{1,0:T(8,128)S(1)}, f32[312,128]{1,0:T(8,128)S(1)}, u32[]{:S(2)}, u32[]{:S(2)}) collective-permute-start(f32[312,128]{1,0:T(8,128)S(1)} %get-tuple-element.18), channel_id=1, source_target_pairs={{0,1},{1,0},{2,3},{3,2},{4,5},{5,4},{6,7},{7,6},{8,9},{9,8},{10,11... | collective-permute-start | bytes 479240 | tf_op jit(solution)/shard_map/ppermute | solution.py:352
  15.0 10.2 %collective-permute-start.1 = (f32[128,384]{1,0:T(8,128)S(1)}, f32[128,384]{1,0:T(8,128)S(1)}, u32[]{:S(2)}, u32[]{:S(2)}) collective-permute-start(f32[128,384]{1,0:T(8,128)S(1)} %add.12), channel_id=1, source_target_pairs={{0,3},{1,2},{2,1},{3,0},{4,7},{5,6},{6,5},{7,4},{8,11},{9,10},{10,... | collective-permute-start | bytes 589832 | tf_op jit(solution)/shard_map/ppermute | solution.py:352
  19.1 12.3 %collective-permute-start.4 = (f32[312,128]{1,0:T(8,128)S(1)}, f32[312,128]{1,0:T(8,128)S(1)}, u32[]{:S(2)}, u32[]{:S(2)}) collective-permute-start(f32[312,128]{1,0:T(8,128)S(1)} %add.14), channel_id=1, source_target_pairs={{0,3},{1,2},{2,1},{3,0},{4,7},{5,6},{6,5},{7,4},{8,11},{9,10},{10,... | collective-permute-start | bytes 479240 | tf_op jit(solution)/shard_map/ppermute | solution.py:352
  25.2 22.8 %collective-permute-start.2 = (f32[128,384]{1,0:T(8,128)S(1)}, f32[128,384]{1,0:T(8,128)S(1)}, u32[]{:S(2)}, u32[]{:S(2)}) collective-permute-start(f32[128,384]{1,0:T(8,128)S(1)} %add.13.mine_ref), channel_id=1, source_target_pairs={{0,1},{1,0},{2,3},{3,2},{4,5},{5,4},{6,7},{7,6},{8,9},{9,8},{10,11... | collective-permute-start | bytes 589832 | tf_op jit(solution)/shard_map/ppermute | solution.py:352
  31.5 6.2 %collective-permute-start.5 = (f32[312,128]{1,0:T(8,128)S(1)}, f32[312,128]{1,0:T(8,128)S(1)}, u32[]{:S(2)}, u32[]{:S(2)}) collective-permute-start(f32[312,128]{1,0:T(8,128)S(1)} %add.15.mine_ref), channel_id=1, source_target_pairs={{0,1},{1,0},{2,3},{3,2},{4,5},{5,4},{6,7},{7,6},{8,9},{9,8},{10,11... | collective-permute-start | bytes 479240 | tf_op jit(solution)/shard_map/ppermute | solution.py:352
